TPU v7x, 32 devices: a whole 2x2x4 slice. The times are simulated.
32 devices in a mesh: row: 4 (over x, core), col: 4 (over z), head: 2 (over y).
Axes of the slice: x: 2, y: 2, z: 4, core: 2. Of those that a mesh axis runs over, the one named last changes fastest.
Arguments:
- query_map: bfloat16 [64, 128, 3072], P('row', 'col', 'head'), may hold values from -6 to 6
- key_map: bfloat16 [64, 128, 3072], P('row', 'col', 'head'), may hold values from -7 to 7
- value_map: bfloat16 [64, 128, 3072], P('row', 'col', 'head'), may hold values from -6 to 6
- window_mask: int32 [4, 4, 13, 13], P('row', 'col'), may hold values 0 or 1
- tile_radius: int32 [4, 4], P('row', 'col'), may hold values from 3 to 6, as said below
- dilation_per_tile: int32 [4, 4], P('row', 'col'), may hold values from 1 to 3, as said below
- rel_bias: float32 [48, 13, 13], P('head'), may hold values from -4 to 4
- out_weight: bfloat16 [3072, 3072], P('head'), may hold values from -0.109375 to 0.109375
Outputs:
- mixed: bfloat16 [64, 128, 3072], P('row', 'col', 'head')
Inputs may be any that keep to these rules, and one draw needn't show every extreme that they name: `tile_radius`: in each row of tiles, at least one tile has radius 6 and dilation 3. `dilation_per_tile`: in each row of tiles, at least one tile has radius 6 and dilation 3.
All inputs are finite; a program needn't handle non-finite values. No bound on the sum of `window_mask` on one device may be relied on, other than what follows from the above.
Results may differ from a plain program's by a relative error of at most 0.0073.
Values may be sent and summed in bfloat16 or wider, within the bound.
A program may use at most 384 MiB of HBM per device.

v0:
```python
import functools
import math

import jax
import jax.numpy as jnp
from jax import lax
from jax.experimental import pallas as pl
from jax.experimental.pallas import tpu as pltpu
from jax.sharding import PartitionSpec as P

HEAD_DIM = 64
RADIUS_MAX = 6
WINDOW = 13
HALO = 18
GROUP = 4
GROUP_FEATURES = GROUP * HEAD_DIM
MASKED = -1e30


def shifted(value, axis, steps):
    count = lax.axis_size(axis)
    first, last = (max(0, -steps), min(count, count - steps))
    return lax.ppermute(value, axis, [(source, source + steps) for source in range(first, last)])


def attention_kernel(
    rows, first_row, dilation_ref, q_ref, *refs
):
    pieces, (spot_ref, table_ref, row_ref, out_ref, kv_ref, bias_ref) = refs[:5], refs[5:]
    dilation = dilation_ref[0]
    cols = q_ref.shape[1]
    lane_head = lax.broadcasted_iota(jnp.int32, (cols, GROUP_FEATURES), 1) // HEAD_DIM

    filled = pieces[0].shape[2]
    tail = filled // 16 * 16
    top = 0
    for piece in pieces:
        count = piece.shape[1]
        for which in range(2):
            kv_ref[which, top : top + count, tail:] = jnp.zeros(
                (count, kv_ref.shape[2] - tail, GROUP_FEATURES), jnp.bfloat16
            )
            kv_ref[which, top : top + count, :filled] = piece[which]
        top += count
    spot = spot_ref[...]
    for h in range(GROUP):
        table = jnp.full(spot.shape, MASKED, jnp.float32)
        for b in range(WINDOW):
            table = jnp.where(spot == b, table_ref[h, b : b + 1, :], table)
        bias_ref[h * cols : (h + 1) * cols] = table

    def one_row(i, carry):
        query = q_ref[i] * jnp.bfloat16(1.0 / math.sqrt(HEAD_DIM))
        zero = jnp.zeros_like(query)
        stacked = jnp.concatenate(
            [jnp.where(lane_head == h, query, zero) for h in range(GROUP)], axis=0
        )
        places = [i + first_row + HALO + (a - RADIUS_MAX) * dilation for a in range(WINDOW)]
        keys = jnp.concatenate([kv_ref[0, place] for place in places], axis=0)
        scores = lax.dot_general(
            stacked, keys, (((1,), (1,)), ((), ())), preferred_element_type=jnp.float32
        )
        scores = scores + bias_ref[...] + row_ref[pl.ds(i, 1), :]
        peak = jnp.max(scores, axis=1, keepdims=True)
        exponent = jnp.exp(scores - peak)
        total = jnp.sum(exponent, axis=1, keepdims=True)
        values = jnp.concatenate([kv_ref[1, place] for place in places], axis=0)
        summed = jnp.dot(
            exponent.astype(jnp.bfloat16), values, preferred_element_type=jnp.float32
        )
        summed = summed / total
        result = summed[:cols]
        for h in range(1, GROUP):
            result = jnp.where(lane_head == h, summed[h * cols : (h + 1) * cols], result)
        out_ref[i] = result.astype(jnp.bfloat16)
        return carry

    lax.fori_loop(0, rows, one_row, 0)


def attend(dilation, query, pieces, spot, table, row_bias, first_group, groups, part, parts):
    tile_rows, cols, _ = query.shape
    rows = tile_rows // parts
    depth = spot.shape[1]
    key_cols = depth // WINDOW
    span_rows = sum(piece.shape[1] for piece in pieces)
    stacked = GROUP * cols
    return pl.pallas_call(
        functools.partial(attention_kernel, rows, part * rows),
        grid=(groups,),
        in_specs=[
            pl.BlockSpec(memory_space=pltpu.SMEM),
            pl.BlockSpec((rows, cols, GROUP_FEATURES), lambda g: (part, 0, g + first_group)),
            *[
                pl.BlockSpec((*piece.shape[:3], GROUP_FEATURES), lambda g: (0, 0, 0, g))
                for piece in pieces
            ],
            pl.BlockSpec((cols, depth), lambda g: (0, 0)),
            pl.BlockSpec((GROUP, WINDOW, depth), lambda g: (g + first_group, 0, 0)),
            pl.BlockSpec((rows, depth), lambda g: (part, 0)),
        ],
        out_specs=pl.BlockSpec((rows, cols, GROUP_FEATURES), lambda g: (0, 0, g)),
        out_shape=jax.ShapeDtypeStruct((rows, cols, groups * GROUP_FEATURES), jnp.bfloat16),
        scratch_shapes=[
            pltpu.VMEM((2, span_rows, key_cols, GROUP_FEATURES), jnp.bfloat16),
            pltpu.VMEM((stacked, depth), jnp.float32),
        ],
        compiler_params=pltpu.CompilerParams(vmem_limit_bytes=40 * 1024 * 1024),
        cost_estimate=pl.CostEstimate(
            flops=groups * rows * 12 * stacked * depth * GROUP_FEATURES,
            bytes_accessed=sum(piece.size for piece in pieces) * 2,
            transcendentals=groups * rows * stacked * depth,
        ),
    )(dilation, query, *pieces, spot, table, row_bias)


def bias_parts(rel_bias, pattern, radius, dilation, tile_rows, tile_cols, key_cols):
    heads = rel_bias.shape[0]
    depth = WINDOW * key_cols
    total_rows = tile_rows * lax.axis_size("row")
    total_cols = tile_cols * lax.axis_size("col")
    row_anchor = lax.axis_index("row") * tile_rows
    col_anchor = lax.axis_index("col") * tile_cols
    steps = jnp.arange(WINDOW, dtype=jnp.int32) - RADIUS_MAX
    spot = lax.broadcasted_iota(jnp.int32, (tile_cols, depth), 1) % key_cols
    column = lax.broadcasted_iota(jnp.int32, (tile_cols, depth), 0)
    offset = jnp.where(
        spot < tile_cols, spot, jnp.where(spot < tile_cols + HALO, spot - tile_cols - HALO, spot - HALO)
    )
    real = spot < tile_cols + 2 * HALO
    global_col = col_anchor + offset
    inside = real & (global_col >= 0) & (global_col < total_cols)
    step_of = jnp.full((tile_cols, depth), -1, jnp.int32)
    for b in range(WINDOW):
        hit = (offset - column == (b - RADIUS_MAX) * dilation) & inside
        step_of = jnp.where(hit, b, step_of)
    chosen = (pattern == 1) | ((steps[:, None] == 0) & (steps[None, :] == 0))
    chosen = chosen & (jnp.abs(steps)[:, None] <= radius) & (jnp.abs(steps)[None, :] <= radius)
    table = jnp.where(chosen[None], rel_bias, MASKED).transpose(0, 2, 1)
    table = jnp.broadcast_to(table[..., None], (heads, WINDOW, WINDOW, key_cols))
    row_step = lax.broadcasted_iota(jnp.int32, (tile_rows, depth), 1) // key_cols - RADIUS_MAX
    row_global = (
        row_anchor + lax.broadcasted_iota(jnp.int32, (tile_rows, depth), 0) + row_step * dilation
    )
    row_fine = (row_global >= 0) & (row_global < total_rows)
    row_bias = jnp.where(row_fine, 0.0, MASKED).astype(jnp.float32)
    return step_of, table.reshape(heads, WINDOW, depth), row_bias


def shards(
    query_map, key_map, value_map, window_mask, tile_radius, dilation_per_tile, rel_bias, out_weight
):
    tile_rows, tile_cols, features = query_map.shape
    key_cols = -(-(tile_cols + 2 * HALO) // 16) * 16
    dilation = dilation_per_tile[0, 0]
    spot, table, row_bias = bias_parts(
        rel_bias, window_mask[0, 0], tile_radius[0, 0], dilation, tile_rows, tile_cols, key_cols
    )
    groups = features // GROUP_FEATURES
    chunks = 2 if groups % 2 == 0 else 1
    spill = HALO - tile_rows
    width = features // chunks
    per_chunk = groups // chunks
    parts = 2 if tile_rows % 16 == 0 else 1
    tokens = tile_rows * tile_cols // parts
    blocks = [[] for _ in range(parts)]
    for c in range(chunks):
        cut = slice(c * width, (c + 1) * width)
        pair = jnp.stack([key_map[..., cut], value_map[..., cut]])
        left = shifted(pair[:, :, tile_cols - HALO :], "col", 1)
        right = shifted(pair[:, :, :HALO], "col", -1)
        wide = jnp.concatenate([pair, left, right], axis=2)
        pieces = [
            shifted(wide[:, tile_rows - spill :], "row", 2),
            shifted(wide, "row", 1),
            wide,
            shifted(wide, "row", -1),
            shifted(wide[:, :spill], "row", -2),
        ]
        split = parts if c == chunks - 1 else 1
        outs = [
            attend(
                dilation.reshape(1), query_map, pieces, spot, table, row_bias,
                c * per_chunk, per_chunk, part, split,
            ).reshape(-1, width)
            for part in range(split)
        ]
        for part in range(parts):
            if split == parts:
                blocks[part].append(outs[part])
            else:
                blocks[part].append(outs[0][part * tokens : (part + 1) * tokens])
    attended = [jnp.concatenate(block, axis=1) for block in blocks]
    count = lax.axis_size("head")
    model = out_weight.shape[1]
    if count != 2:
        partials = jnp.dot(
            jnp.concatenate(attended), out_weight, preferred_element_type=jnp.float32
        )
        mixed = lax.psum_scatter(partials, "head", scatter_dimension=1, tiled=True)
        return mixed.astype(jnp.bfloat16).reshape(tile_rows, tile_cols, model // count)
    me = lax.axis_index("head")
    half = model // 2
    theirs = lax.dynamic_slice_in_dim(out_weight, (1 - me) * half, half, 1)
    mine = lax.dynamic_slice_in_dim(out_weight, me * half, half, 1)
    mixed = []
    for block in attended:
        sent = jnp.dot(block, theirs, preferred_element_type=jnp.float32).astype(jnp.bfloat16)
        got = lax.ppermute(sent, "head", [(0, 1), (1, 0)])
        kept = jnp.dot(block, mine, preferred_element_type=jnp.float32)
        mixed.append((kept + got.astype(jnp.float32)).astype(jnp.bfloat16))
    return jnp.concatenate(mixed).reshape(tile_rows, tile_cols, half)


def solution(mesh):
    placed = (
        P("row", "col", "head"),
        P("row", "col", "head"),
        P("row", "col", "head"),
        P("row", "col", None, None),
        P("row", "col"),
        P("row", "col"),
        P("head", None, None),
        P("head", None),
    )
    return jax.shard_map(
        shards, mesh=mesh, in_specs=placed, out_specs=P("row", "col", "head"), check_vma=False
    )
```

profile of v0, /device:TPU:0, one launch (start us, length us, event | category | flops | bytes accessed | tf_op | source)
XLA Modules:
  0.0 250.1 jit_solution(13801900371159752499)
XLA Ops:
  0.0 2.0 slice_bitcast_fusion.2
  2.8 1.3 collective-permute-start.1
  4.2 5.6 %collective-permute-start = (bf16[2,16,18,768]{3,1,2,0:T(8,128)(2,1)S(1)}, bf16[2,16,18,768]{3,1,2,0:T(8,128)(2,1)S(1)}, u32[]{:S(2)}, u32[]{:S(2)}) collective-permute-start(bf16[2,16,18,768]{3,1,2,0:T(8,128)(2,1)S(1)} %copy.14), channel_id=1, source_target_pairs={{0,2},{2,4},{4,6},{1,3},{3,5},{5,7},{8,10},{10,12},{12,14},{9,11},... | collective-permute-start | bytes 2654216 | tf_op jit(solution)/shard_map/ppermute | solution.py:23
  9.9 17.5 %collective-permute-done.1 = bf16[2,16,18,768]{3,1,2,0:T(8,128)(2,1)S(1)} collective-permute-done((bf16[2,16,18,768]{3,1,2,0:T(8,128)(2,1)S(1)}, bf16[2,16,18,768]{3,1,2,0:T(8,128)(2,1)S(1)}, u32[]{:S(2)}, u32[]{:S(2)}) %collective-permute-start.1) | collective-permute-done | bytes 884768 | tf_op jit(solution)/shard_map/ppermute | solution.py:23
  27.6 1.1 collective-permute-done
  29.0 1.0 pad_maximum_fusion.refs_2_
  30.0 2.5 copy.18
  32.4 1.3 collective-permute-start.4
  33.7 4.9 %collective-permute-start.3 = (bf16[2,16,68,768]{3,1,2,0:T(8,128)(2,1)}, bf16[2,16,68,768]{3,1,2,0:T(8,128)(2,1)}, u32[]{:S(2)}, u32[]{:S(2)}) collective-permute-start(bf16[2,16,68,768]{3,1,2,0:T(8,128)(2,1)} %copy.18), channel_id=1, source_target_pairs={{0,8},{8,16},{16,24},{1,9},{9,17},{17,25},{2,10},{10,18},{18,26},{... | collective-permute-start | bytes 10027016 | tf_op jit(solution)/shard_map/ppermute | solution.py:23
  39.1 1.1 copy.25
  40.2 1.3 collective-permute-start.7
  41.5 1.1 copy.24
  42.6 5.9 %collective-permute-start.6 = (bf16[2,16,18,768]{3,1,2,0:T(8,128)(2,1)}, bf16[2,16,18,768]{3,1,2,0:T(8,128)(2,1)}, u32[]{:S(2)}, u32[]{:S(2)}) collective-permute-start(bf16[2,16,18,768]{3,1,2,0:T(8,128)(2,1)} %copy.24), channel_id=1, source_target_pairs={{0,2},{2,4},{4,6},{1,3},{3,5},{5,7},{8,10},{10,12},{12,14},{9,11},... | collective-permute-start | bytes 2654216 | tf_op jit(solution)/shard_map/ppermute | solution.py:23
  50.6 13.5 %collective-permute-done.7 = bf16[2,16,18,768]{3,1,2,0:T(8,128)(2,1)} collective-permute-done((bf16[2,16,18,768]{3,1,2,0:T(8,128)(2,1)}, bf16[2,16,18,768]{3,1,2,0:T(8,128)(2,1)}, u32[]{:S(2)}, u32[]{:S(2)}) %collective-permute-start.7) | collective-permute-done | bytes 884768 | tf_op jit(solution)/shard_map/ppermute | solution.py:23
  64.2 1.4 copy.27
  65.6 0.8 collective-permute-done.6
  66.4 1.4 copy.26
  67.9 1.0 pad_maximum_fusion.1.refs_2_
  68.9 2.8 %copy.28 = bf16[2,16,68,768]{3,1,2,0:T(8,128)(2,1)} copy(bf16[2,16,68,768]{3,2,1,0:T(8,128)(2,1)S(1)} %pad_maximum_fusion.1.refs_2_) | data formatting | bytes 6684672 | tf_op jit(solution)/shard_map/concatenate | solution.py:172
  71.7 1.3 collective-permute-start.10
  73.0 4.8 %collective-permute-start.9 = (bf16[2,16,68,768]{3,1,2,0:T(8,128)(2,1)}, bf16[2,16,68,768]{3,1,2,0:T(8,128)(2,1)}, u32[]{:S(2)}, u32[]{:S(2)}) collective-permute-start(bf16[2,16,68,768]{3,1,2,0:T(8,128)(2,1)} %copy.28), channel_id=1, source_target_pairs={{0,8},{8,16},{16,24},{1,9},{9,17},{17,25},{2,10},{10,18},{18,26},{... | collective-permute-start | bytes 10027016 | tf_op jit(solution)/shard_map/ppermute | solution.py:23
  77.8 1.0 select_select_fusion.1.refs_5_
  78.8 1.0 fusion.52
  79.8 1.3 collective-permute-start.5
  81.1 6.1 %collective-permute-start.2 = (bf16[2,2,68,768]{3,2,1,0:T(8,128)(2,1)}, bf16[2,2,68,768]{3,2,1,0:T(8,128)(2,1)}, u32[]{:S(2)}, u32[]{:S(2)}) collective-permute-start(bf16[2,2,68,768]{3,2,1,0:T(8,128)(2,1)} %get-tuple-element.6), channel_id=1, source_target_pairs={{0,16},{8,24},{1,17},{9,25},{2,18},{10,26},{3,19},{11,27},{4,20},{... | collective-permute-start | bytes 1253384 | tf_op jit(solution)/shard_map/ppermute | solution.py:23
  87.3 0.8 select_bitcast_fusion
  88.0 1.7 copy.20
  89.7 2.8 %broadcast_in_dim.87 = f32[24,13,13,80]{3,2,0,1:T(8,128)} broadcast(f32[24,13,13]{2,0,1:T(8,128)} %copy.20), dimensions={0,1,2} | broadcast | bytes 1314144 | tf_op jit(solution)/shard_map/broadcast_in_dim | solution.py:140
  92.5 3.2 %reshape.101 = f32[24,13,1040]{2,0,1:T(8,128)} reshape(f32[24,13,13,80]{3,2,0,1:T(8,128)} %broadcast_in_dim.87) | data formatting | bytes 2595840 | tf_op jit(solution)/shard_map/reshape | solution.py:147
  95.7 2.9 %copy.23.refs_6_ = f32[24,13,1040]{2,1,0:T(8,128)} copy(f32[24,13,1040]{2,0,1:T(8,128)} %reshape.101) | data formatting | bytes 2595840 | tf_op jit(solution)/shard_map/reshape | solution.py:147
  98.6 1.2 fusion.53
  99.8 4.9 %copy.22.refs_3_ = bf16[2,16,68,768]{3,2,1,0:T(8,128)(2,1)} copy(bf16[2,16,68,768]{3,1,2,0:T(8,128)(2,1)} %collective-permute-done.4) | data formatting | bytes 6684672 | tf_op jit(solution)/shard_map/ppermute | solution.py:23
  104.7 1.6 collective-permute-start.11
  106.3 3.1 %copy.21.refs_1_ = bf16[2,16,68,768]{3,2,1,0:T(8,128)(2,1)S(1)} copy(bf16[2,16,68,768]{3,1,2,0:T(8,128)(2,1)} %collective-permute-done.3) | data formatting | bytes 6684672 | tf_op jit(solution)/shard_map/ppermute | solution.py:23
  109.3 17.5 %collective-permute-done.5.refs_4_ = bf16[2,2,68,768]{3,2,1,0:T(8,128)(2,1)} collective-permute-done((bf16[2,2,68,768]{3,2,1,0:T(8,128)(2,1)}, bf16[2,2,68,768]{3,2,1,0:T(8,128)(2,1)}, u32[]{:S(2)}, u32[]{:S(2)}) %collective-permute-start.5) | collective-permute-done | bytes 417824 | tf_op jit(solution)/shard_map/ppermute | solution.py:23
  126.9 1.6 collective-permute-start.8
  128.6 42.1 %shard_map.82 = bf16[16,32,768]{2,1,0:T(8,128)(2,1)S(1)} custom-call(s32[1]{0:T(128)} %bitcast.27.dilation_ref, bf16[16,32,1536]{2,1,0:T(8,128)(2,1)S(1)} %copy-done.5, bf16[2,2,68,768]{3,2,1,0:T(8,128)(2,1)} %collective-permute-done.2.refs_0_, bf16[2,16,68,768]{3,2,1,0:T(8,128)(2,1)S(1)} %copy.21.refs_1_, ...), custom_call_target="tpu_custom_call" | custom-call | flops 19629342720 | bytes 10862592 | tf_op jit(solution)/shard_map/pallas_call | solution.py:88
  170.7 4.9 %copy.31.refs_3_ = bf16[2,16,68,768]{3,2,1,0:T(8,128)(2,1)} copy(bf16[2,16,68,768]{3,1,2,0:T(8,128)(2,1)} %collective-permute-done.10) | data formatting | bytes 6684672 | tf_op jit(solution)/shard_map/ppermute | solution.py:23
  175.6 3.2 %copy.30.refs_1_ = bf16[2,16,68,768]{3,2,1,0:T(8,128)(2,1)S(1)} copy(bf16[2,16,68,768]{3,1,2,0:T(8,128)(2,1)} %collective-permute-done.9) | data formatting | bytes 6684672 | tf_op jit(solution)/shard_map/ppermute | solution.py:23
  178.9 23.4 %shard_map.83 = bf16[8,32,768]{2,1,0:T(8,128)(2,1)S(1)} custom-call(s32[1]{0:T(128)} %bitcast.28.dilation_ref, bf16[16,32,1536]{2,1,0:T(8,128)(2,1)S(1)} %copy-done.5, bf16[2,2,68,768]{3,2,1,0:T(8,128)(2,1)S(1)} %collective-permute-done.8.refs_0_, bf16[2,16,68,768]{3,2,1,0:T(8,128)(2,1)S(1)} %copy.30.refs_1_, bf16[2,16,68,768]{3,2,1,0:T(8,128)(2,1)S(1)} %copy-done.1, ...), custom_call_target="tpu_custom_call" | custom-call | flops 9814671360 | bytes 10862592 | tf_op jit(solution)/shard_map/pallas_call | solution.py:88
  202.3 1.4 fusion.20
  203.7 1.7 collective-permute-start.12
  205.4 23.2 %shard_map.84 = bf16[8,32,768]{2,1,0:T(8,128)(2,1)S(1)} custom-call(s32[1]{0:T(128)} %bitcast.29.dilation_ref, bf16[16,32,1536]{2,1,0:T(8,128)(2,1)S(1)} %copy-done.5, bf16[2,2,68,768]{3,2,1,0:T(8,128)(2,1)S(1)} %collective-permute-done.8.refs_0_, bf16[2,16,68,768]{3,2,1,0:T(8,128)(2,1)S(1)} %copy.30.refs_1_, bf16[2,16,68,768]{3,2,1,0:T(8,128)(2,1)S(1)} %copy-done.1, ...), custom_call_target="tpu_custom_call" | custom-call | flops 9814671360 | bytes 10862592 | tf_op jit(solution)/shard_map/pallas_call | solution.py:88
  228.6 2.3 fusion.23
  231.4 3.7 %fusion.17 = bf16[256,1536]{1,0:T(8,128)(2,1)S(1)} fusion(bf16[1536,3072]{1,0:T(8,128)(2,1)} %param.15, s32[]{:T(128)S(6)} %select_n.172, bf16[256,1536]{1,0:T(8,128)(2,1)S(1)} %collective-permute-done.12, bf16[256,768]{1,0:T(8,128)(2,1)S(1)} %bitcast.46, bf16[256,768]{1,0:T(8,128)(2,1)S(1)} %bitcast.50), kind=kOutput, calls=%fused_computation.13 | convolution fusion | flops 1210712064 | bytes 7077892 | tf_op jit(solution)/shard_map/dot_general | solution.py:210
  235.1 9.8 %collective-permute-done.13 = bf16[256,1536]{1,0:T(8,128)(2,1)} collective-permute-done((bf16[256,1536]{1,0:T(8,128)(2,1)}, bf16[256,1536]{1,0:T(8,128)(2,1)}, u32[]{:S(2)}, u32[]{:S(2)}) %collective-permute-start.13) | collective-permute-done | bytes 786464 | tf_op jit(solution)/shard_map/ppermute | solution.py:209
  244.9 3.9 %fusion.14 = bf16[256,1536]{1,0:T(8,128)(2,1)S(1)} fusion(bf16[1536,3072]{1,0:T(8,128)(2,1)} %param.15, s32[]{:T(128)S(6)} %select_n.172, bf16[256,1536]{1,0:T(8,128)(2,1)} %collective-permute-done.13, bf16[256,768]{1,0:T(8,128)(2,1)S(1)} %bitcast.44, bf16[256,768]{1,0:T(8,128)(2,1)S(1)} %bitcast.48), kind=kOutput, calls=%fused_computation.12 | convolution fusion | flops 1210712064 | bytes 7077892 | tf_op jit(solution)/shard_map/dot_general | solution.py:210
  248.9 1.2 pad_maximum_fusion.2
  (56 shorter events, 3.4 us)
Async XLA Ops:
  2.1 36.5 %copy-start.6 = (bf16[1,16,32,768]{3,2,1,0:T(8,128)(2,1)}, bf16[1,16,32,768]{3,2,1,0:T(8,128)(2,1)S(1)}, u32[]{:S(2)}) copy-start(bf16[1,16,32,768]{3,2,1,0:T(8,128)(2,1)S(1)} %get-tuple-element.14) | copy-start | bytes 2359300
  2.1 36.5 %copy-start.8 = (bf16[1,16,32,768]{3,2,1,0:T(8,128)(2,1)}, bf16[1,16,32,768]{3,2,1,0:T(8,128)(2,1)S(1)}, u32[]{:S(2)}) copy-start(bf16[1,16,32,768]{3,2,1,0:T(8,128)(2,1)S(1)} %get-tuple-element.19) | copy-start | bytes 2359300
  2.8 24.6 %collective-permute-start.1 = (bf16[2,16,18,768]{3,1,2,0:T(8,128)(2,1)S(1)}, bf16[2,16,18,768]{3,1,2,0:T(8,128)(2,1)S(1)}, u32[]{:S(2)}, u32[]{:S(2)}) collective-permute-start(bf16[2,16,18,768]{3,1,2,0:T(8,128)(2,1)S(1)} %copy.15), channel_id=1, source_target_pairs={{2,0},{4,2},{6,4},{3,1},{5,3},{7,5},{10,8},{12,10},{14,12},{11,9},... | collective-permute-start | bytes 2654216 | tf_op jit(solution)/shard_map/ppermute | solution.py:23
  4.2 24.5 %collective-permute-start = (bf16[2,16,18,768]{3,1,2,0:T(8,128)(2,1)S(1)}, bf16[2,16,18,768]{3,1,2,0:T(8,128)(2,1)S(1)}, u32[]{:S(2)}, u32[]{:S(2)}) collective-permute-start(bf16[2,16,18,768]{3,1,2,0:T(8,128)(2,1)S(1)} %copy.14), channel_id=1, source_target_pairs={{0,2},{2,4},{4,6},{1,3},{3,5},{5,7},{8,10},{10,12},{12,14},{9,11},... | collective-permute-start | bytes 2654216 | tf_op jit(solution)/shard_map/ppermute | solution.py:23
  32.4 48.7 %collective-permute-start.4 = (bf16[2,16,68,768]{3,1,2,0:T(8,128)(2,1)}, bf16[2,16,68,768]{3,1,2,0:T(8,128)(2,1)}, u32[]{:S(2)}, u32[]{:S(2)}) collective-permute-start(bf16[2,16,68,768]{3,1,2,0:T(8,128)(2,1)} %copy.18), channel_id=1, source_target_pairs={{8,0},{16,8},{24,16},{9,1},{17,9},{25,17},{10,2},{18,10},{26,18},{... | collective-permute-start | bytes 10027016 | tf_op jit(solution)/shard_map/ppermute | solution.py:23
  33.7 71.0 %collective-permute-start.3 = (bf16[2,16,68,768]{3,1,2,0:T(8,128)(2,1)}, bf16[2,16,68,768]{3,1,2,0:T(8,128)(2,1)}, u32[]{:S(2)}, u32[]{:S(2)}) collective-permute-start(bf16[2,16,68,768]{3,1,2,0:T(8,128)(2,1)} %copy.18), channel_id=1, source_target_pairs={{0,8},{8,16},{16,24},{1,9},{9,17},{17,25},{2,10},{10,18},{18,26},{... | collective-permute-start | bytes 10027016 | tf_op jit(solution)/shard_map/ppermute | solution.py:23
  39.1 10.8 %copy-start.11 = (s32[1,1,13,13]{3,1,2,0:T(1,128)S(1)}, s32[1,1,13,13]{3,1,2,0:T(1,128)}, u32[]{:S(2)}) copy-start(s32[1,1,13,13]{3,1,2,0:T(1,128)} %param.11) | copy-start | bytes 2032
  40.2 24.0 %collective-permute-start.7 = (bf16[2,16,18,768]{3,1,2,0:T(8,128)(2,1)}, bf16[2,16,18,768]{3,1,2,0:T(8,128)(2,1)}, u32[]{:S(2)}, u32[]{:S(2)}) collective-permute-start(bf16[2,16,18,768]{3,1,2,0:T(8,128)(2,1)} %copy.25), channel_id=1, source_target_pairs={{2,0},{4,2},{6,4},{3,1},{5,3},{7,5},{10,8},{12,10},{14,12},{11,9},... | collective-permute-start | bytes 2654216 | tf_op jit(solution)/shard_map/ppermute | solution.py:23
  42.6 23.8 %collective-permute-start.6 = (bf16[2,16,18,768]{3,1,2,0:T(8,128)(2,1)}, bf16[2,16,18,768]{3,1,2,0:T(8,128)(2,1)}, u32[]{:S(2)}, u32[]{:S(2)}) collective-permute-start(bf16[2,16,18,768]{3,1,2,0:T(8,128)(2,1)} %copy.24), channel_id=1, source_target_pairs={{0,2},{2,4},{4,6},{1,3},{3,5},{5,7},{8,10},{10,12},{12,14},{9,11},... | collective-permute-start | bytes 2654216 | tf_op jit(solution)/shard_map/ppermute | solution.py:23
  49.8 18.1 %copy-start.7 = (bf16[1,16,32,768]{3,2,1,0:T(8,128)(2,1)S(1)}, bf16[1,16,32,768]{3,2,1,0:T(8,128)(2,1)}, u32[]{:S(2)}) copy-start(bf16[1,16,32,768]{3,2,1,0:T(8,128)(2,1)} %copy-done.6) | copy-start | bytes 2359300
  49.8 18.1 %copy-start.9 = (bf16[1,16,32,768]{3,2,1,0:T(8,128)(2,1)S(1)}, bf16[1,16,32,768]{3,2,1,0:T(8,128)(2,1)}, u32[]{:S(2)}) copy-start(bf16[1,16,32,768]{3,2,1,0:T(8,128)(2,1)} %copy-done.8) | copy-start | bytes 2359300
  68.9 2.8 %copy-start = (bf16[2,16,68,768]{3,2,1,0:T(8,128)(2,1)}, bf16[2,16,68,768]{3,2,1,0:T(8,128)(2,1)S(1)}, u32[]{:S(2)}) copy-start(bf16[2,16,68,768]{3,2,1,0:T(8,128)(2,1)S(1)} %pad_maximum_fusion.1.refs_2_) | copy-start | bytes 10027012
  68.9 18.4 %copy-start.10 = (f32[24,13,13]{0,2,1:T(8,128)S(1)}, f32[24,13,13]{0,2,1:T(8,128)}, u32[]{:S(2)}) copy-start(f32[24,13,13]{0,2,1:T(8,128)} %param.14) | copy-start | bytes 48676
  71.7 99.0 %collective-permute-start.10 = (bf16[2,16,68,768]{3,1,2,0:T(8,128)(2,1)}, bf16[2,16,68,768]{3,1,2,0:T(8,128)(2,1)}, u32[]{:S(2)}, u32[]{:S(2)}) collective-permute-start(bf16[2,16,68,768]{3,1,2,0:T(8,128)(2,1)} %copy.28), channel_id=1, source_target_pairs={{8,0},{16,8},{24,16},{9,1},{17,9},{25,17},{10,2},{18,10},{26,18},{... | collective-permute-start | bytes 10027016 | tf_op jit(solution)/shard_map/ppermute | solution.py:23
  73.0 102.6 %collective-permute-start.9 = (bf16[2,16,68,768]{3,1,2,0:T(8,128)(2,1)}, bf16[2,16,68,768]{3,1,2,0:T(8,128)(2,1)}, u32[]{:S(2)}, u32[]{:S(2)}) collective-permute-start(bf16[2,16,68,768]{3,1,2,0:T(8,128)(2,1)} %copy.28), channel_id=1, source_target_pairs={{0,8},{8,16},{16,24},{1,9},{9,17},{17,25},{2,10},{10,18},{18,26},{... | collective-permute-start | bytes 10027016 | tf_op jit(solution)/shard_map/ppermute | solution.py:23
  79.8 47.1 %collective-permute-start.5 = (bf16[2,2,68,768]{3,2,1,0:T(8,128)(2,1)}, bf16[2,2,68,768]{3,2,1,0:T(8,128)(2,1)}, u32[]{:S(2)}, u32[]{:S(2)}) collective-permute-start(bf16[2,2,68,768]{3,2,1,0:T(8,128)(2,1)} %get-tuple-element.5), channel_id=1, source_target_pairs={{16,0},{24,8},{17,1},{25,9},{18,2},{26,10},{19,3},{27,11},{20,4},{... | collective-permute-start | bytes 1253384 | tf_op jit(solution)/shard_map/ppermute | solution.py:23
  81.1 47.4 %collective-permute-start.2 = (bf16[2,2,68,768]{3,2,1,0:T(8,128)(2,1)}, bf16[2,2,68,768]{3,2,1,0:T(8,128)(2,1)}, u32[]{:S(2)}, u32[]{:S(2)}) collective-permute-start(bf16[2,2,68,768]{3,2,1,0:T(8,128)(2,1)} %get-tuple-element.6), channel_id=1, source_target_pairs={{0,16},{8,24},{1,17},{9,25},{2,18},{10,26},{3,19},{11,27},{4,20},{... | collective-permute-start | bytes 1253384 | tf_op jit(solution)/shard_map/ppermute | solution.py:23
  104.7 23.9 %copy-start.2 = (f32[24,13,1040]{2,1,0:T(8,128)S(1)}, f32[24,13,1040]{2,1,0:T(8,128)}, u32[]{:S(2)}) copy-start(f32[24,13,1040]{2,1,0:T(8,128)} %copy.23.refs_6_) | copy-start | bytes 3893764
  104.7 23.9 %copy-start.3 = (s32[32,1040]{1,0:T(8,128)S(1)}, s32[32,1040]{1,0:T(8,128)}, u32[]{:S(2)}) copy-start(s32[32,1040]{1,0:T(8,128)} %select_select_fusion.1.refs_5_) | copy-start | bytes 399364
  104.7 23.9 %copy-start.4 = (f32[16,1040]{1,0:T(8,128)S(1)}, f32[16,1040]{1,0:T(8,128)}, u32[]{:S(2)}) copy-start(f32[16,1040]{1,0:T(8,128)} %fusion.34.refs_7_) | copy-start | bytes 199684
  104.7 23.9 %copy-start.5 = (bf16[16,32,1536]{2,1,0:T(8,128)(2,1)S(1)}, bf16[16,32,1536]{2,1,0:T(8,128)(2,1)}, u32[]{:S(2)}) copy-start(bf16[16,32,1536]{2,1,0:T(8,128)(2,1)} %q_ref.5) | copy-start | bytes 4718596
  104.7 74.1 %collective-permute-start.11 = (bf16[2,2,68,768]{3,2,1,0:T(8,128)(2,1)S(1)}, bf16[2,2,68,768]{3,2,1,0:T(8,128)(2,1)S(1)}, u32[]{:S(2)}, u32[]{:S(2)}) collective-permute-start(bf16[2,2,68,768]{3,2,1,0:T(8,128)(2,1)S(1)} %get-tuple-element.7), channel_id=1, source_target_pairs={{16,0},{24,8},{17,1},{25,9},{18,2},{26,10},{19,3},{27,11},{20,4},{... | collective-permute-start | bytes 1253384 | tf_op jit(solution)/shard_map/ppermute | solution.py:23
  126.9 52.0 %collective-permute-start.8 = (bf16[2,2,68,768]{3,2,1,0:T(8,128)(2,1)S(1)}, bf16[2,2,68,768]{3,2,1,0:T(8,128)(2,1)S(1)}, u32[]{:S(2)}, u32[]{:S(2)}) collective-permute-start(bf16[2,2,68,768]{3,2,1,0:T(8,128)(2,1)S(1)} %get-tuple-element.8), channel_id=1, source_target_pairs={{0,16},{8,24},{1,17},{9,25},{2,18},{10,26},{3,19},{11,27},{4,20},{... | collective-permute-start | bytes 1253384 | tf_op jit(solution)/shard_map/ppermute | solution.py:23
  175.5 3.3 %copy-start.1 = (bf16[2,16,68,768]{3,2,1,0:T(8,128)(2,1)S(1)}, bf16[2,16,68,768]{3,2,1,0:T(8,128)(2,1)}, u32[]{:S(2)}) copy-start(bf16[2,16,68,768]{3,2,1,0:T(8,128)(2,1)} %copy-done) | copy-start | bytes 10027012
  175.6 26.7 %slice-start = ((s8[9437184]{0:T(1024)(128)(4,1)}), s8[1048576]{0:T(1024)(128)(4,1)S(1)}, s32[]{:S(2)}) async-start(s8[9437184]{0:T(1024)(128)(4,1)} %bitcast.51), calls=%async_computation | async-start | bytes 2097152
  178.9 23.4 %slice-start.1 = ((s8[9437184]{0:T(1024)(128)(4,1)}), s8[4194304]{0:T(1024)(128)(4,1)S(1)}, s32[]{:S(2)}) async-start(s8[9437184]{0:T(1024)(128)(4,1)} %bitcast.51), calls=%async_computation.1 | async-start | bytes 8388608
  178.9 23.4 %slice-start.2 = ((s8[9437184]{0:T(1024)(128)(4,1)}), s8[4194304]{0:T(1024)(128)(4,1)S(1)}, s32[]{:S(2)}) async-start(s8[9437184]{0:T(1024)(128)(4,1)} %bitcast.51), calls=%async_computation.2 | async-start | bytes 8388608
  203.7 27.7 %collective-permute-start.12 = (bf16[256,1536]{1,0:T(8,128)(2,1)S(1)}, bf16[256,1536]{1,0:T(8,128)(2,1)S(1)}, u32[]{:S(2)}, u32[]{:S(2)}) collective-permute-start(bf16[256,1536]{1,0:T(8,128)(2,1)S(1)} %fusion.20), channel_id=1, source_target_pairs={{0,1},{1,0},{2,3},{3,2},{4,5},{5,4},{6,7},{7,6},{8,9},{9,8},{10,11... | collective-permute-start | bytes 2359304 | tf_op jit(solution)/shard_map/ppermute | solution.py:209
  230.9 14.1 %collective-permute-start.13 = (bf16[256,1536]{1,0:T(8,128)(2,1)}, bf16[256,1536]{1,0:T(8,128)(2,1)}, u32[]{:S(2)}, u32[]{:S(2)}) collective-permute-start(bf16[256,1536]{1,0:T(8,128)(2,1)} %fusion.23), channel_id=1, source_target_pairs={{0,1},{1,0},{2,3},{3,2},{4,5},{5,4},{6,7},{7,6},{8,9},{9,8},{10,11... | collective-permute-start | bytes 2359304 | tf_op jit(solution)/shard_map/ppermute | solution.py:209
where the time goes:
time: 252 us; the launch traced here: 250 us
  Pallas kernels  88.7 us (35%)
  waiting for transfers between devices  60.3 us (24%)
  local copies, waits for them, and re-layouts  42.2 us (17%)
  starting transfers between devices  39.1 us (16%)
  matrix products  11.3 us (4%)
  other arithmetic  6.83 us (3%)
    pallas_call x3, Pallas kernels, attend(): pl.pallas_call(functools.partial(attention_kernel, rows, part * rows), gr...  88.7 us
    ppermute x12, waiting for transfers between devices, shifted(): lax.ppermute(value, axis, [(source, source + steps) for source in range(f...  50.5 us
    ppermute x12, starting transfers between devices, shifted(): lax.ppermute(value, axis, [(source, source + steps) for source in range(f...  37 us
    ppermute x8, local copies, waits for them, and re-layouts, shifted(): lax.ppermute(value, axis, [(source, source + steps) for source in range(f...  19.5 us
    ppermute x2, waiting for transfers between devices, shards(): got = lax.ppermute(sent, 'head', [(0, 1), (1, 0)])  9.83 us
    dot_general x2, matrix products, shards(): kept = jnp.dot(block, mine, preferred_element_type=jnp.float32)  7.65 us
    reshape x2, local copies, waits for them, and re-layouts, bias_parts(): return (step_of, table.reshape(heads, WINDOW, depth), row_bias)  6.09 us
    concatenate x2, local copies, waits for them, and re-layouts, shards(): wide = jnp.concatenate([pair, left, right], axis=2)  5.24 us
  transfers between devices with their start and end apart: 14, of which 6 were waited for; matrix products, arithmetic and copies ran while one was open for 19% of the time, Pallas kernels for 26%

commit v1 on v0

v1 whole, which is shorter than its diff:
```python
import functools
import math

import jax
import jax.numpy as jnp
from jax import lax
from jax.experimental import pallas as pl
from jax.experimental.pallas import tpu as pltpu
from jax.sharding import PartitionSpec as P

HEAD_DIM = 64
RADIUS_MAX = 6
DILATION_LIMIT = 3
WINDOW = 2 * RADIUS_MAX + 1
HALO = RADIUS_MAX * DILATION_LIMIT
GROUP = 4
GROUP_FEATURES = GROUP * HEAD_DIM
MASKED = -1e30

QUERY_COLS = 4
SLOTS = QUERY_COLS + WINDOW - 1
PAIRS = SLOTS // 2
BIAS_STEPS = SLOTS + QUERY_COLS - 2
TABLE_STEPS = BIAS_STEPS + 1
ENTRY = QUERY_COLS + SLOTS + PAIRS

TO_LEFT, TO_RIGHT, TO_ABOVE, TO_BELOW, TOP_UP, BOTTOM_DOWN = range(6)
MATE_LEFT, MATE_RIGHT, ACROSS_LEFT, ACROSS_RIGHT = range(6, 10)
UP_LEFT, UP_RIGHT, DOWN_LEFT, DOWN_RIGHT = range(10, 14)
COPIES = 14


def block_count(cols):
    return max(
        d * -(-(-(-cols // d)) // QUERY_COLS) for d in range(1, DILATION_LIMIT + 1)
    )


def fused_kernel(
    groups, rows, cols, table_ref, slot_ref, bias_ref, step_ref, spread_ref, query_ref,
    kv_hbm, edge_hbm, out_ref, *scratch
):
    kv_refs, edge_refs = scratch[:groups], scratch[groups : 2 * groups]
    tile_ref, done_ref, send_sems, recv_sems, own_sems = scratch[2 * groups :]
    spill = HALO - rows
    own = slice(HALO, HALO + cols)
    left, right = slice(0, HALO), slice(HALO + cols, cols + 2 * HALO)
    row, col = lax.axis_index("row"), lax.axis_index("col")
    n_row, n_col = lax.axis_size("row"), lax.axis_size("col")
    lower = lax.rem(row, 2)
    mate = row + 1 - 2 * lower
    has_left, has_right = col > 0, col < n_col - 1
    has_above, has_below = row > 0, row < n_row - 1
    has_above2, has_below2 = row > 1, row < n_row - 2
    has_mate = mate < n_row
    has_across = jnp.where(lower == 1, has_below, has_above)
    mate_rows = pl.ds(pl.multiple_of((1 + lower) * rows, rows), rows)
    across_rows = pl.ds(pl.multiple_of((1 + lower) * rows, rows), rows)
    edge = spill * cols
    side = -(-spill * HALO // 16) * 16

    def copy(g, which):
        kv, extra = kv_refs[g], edge_refs[g]
        base = slice(0, rows)
        up, down = slice(rows, 2 * rows), slice(2 * rows, 3 * rows)
        near_left, near_right = slice(HALO, 2 * HALO), slice(cols, cols + HALO)
        source, target, there = {
            TO_LEFT: (kv_hbm.at[g, :, :HALO], kv.at[:, right, base], {"col": col - 1}),
            TO_RIGHT: (kv_hbm.at[g, :, cols - HALO :], kv.at[:, left, base], {"col": col + 1}),
            TO_ABOVE: (kv_hbm.at[g], kv.at[:, own, down], {"row": row - 1}),
            TO_BELOW: (kv_hbm.at[g], kv.at[:, own, up], {"row": row + 1}),
            TOP_UP: (edge_hbm.at[g, :, 0], extra.at[:, 1, :edge], {"row": row - 2}),
            BOTTOM_DOWN: (edge_hbm.at[g, :, 1], extra.at[:, 0, :edge], {"row": row + 2}),
            MATE_LEFT: (kv.at[:, left, base], kv.at[:, left, mate_rows], {"row": mate}),
            MATE_RIGHT: (kv.at[:, right, base], kv.at[:, right, mate_rows], {"row": mate}),
            ACROSS_LEFT: (
                kv.at[:, near_left, across_rows], kv.at[:, right, across_rows], {"col": col - 1}
            ),
            ACROSS_RIGHT: (
                kv.at[:, near_right, across_rows], kv.at[:, left, across_rows], {"col": col + 1}
            ),
            UP_LEFT: (
                extra.at[:, 0, :side], extra.at[:, 0, edge + side : edge + 2 * side], {"col": col - 1}
            ),
            UP_RIGHT: (
                extra.at[:, 0, edge - side : edge], extra.at[:, 0, edge : edge + side], {"col": col + 1}
            ),
            DOWN_LEFT: (
                extra.at[:, 1, :side], extra.at[:, 1, edge + side : edge + 2 * side], {"col": col - 1}
            ),
            DOWN_RIGHT: (
                extra.at[:, 1, edge - side : edge], extra.at[:, 1, edge : edge + side], {"col": col + 1}
            ),
        }[which]
        return pltpu.make_async_remote_copy(
            src_ref=source, dst_ref=target, send_sem=send_sems.at[g, which],
            recv_sem=recv_sems.at[g, which], device_id=there,
            device_id_type=pl.DeviceIdType.MESH,
        )

    sends = {
        TO_LEFT: has_left, TO_RIGHT: has_right, TO_ABOVE: has_above, TO_BELOW: has_below,
        TOP_UP: has_above2, BOTTOM_DOWN: has_below2,
        MATE_LEFT: has_mate & has_left, MATE_RIGHT: has_mate & has_right,
        ACROSS_LEFT: has_across & has_left, ACROSS_RIGHT: has_across & has_right,
        UP_LEFT: has_above2 & has_left, UP_RIGHT: has_above2 & has_right,
        DOWN_LEFT: has_below2 & has_left, DOWN_RIGHT: has_below2 & has_right,
    }
    receives = {
        TO_LEFT: has_right, TO_RIGHT: has_left, TO_ABOVE: has_below, TO_BELOW: has_above,
        TOP_UP: has_below2, BOTTOM_DOWN: has_above2,
        MATE_LEFT: has_mate & has_left, MATE_RIGHT: has_mate & has_right,
        ACROSS_LEFT: has_across & has_right, ACROSS_RIGHT: has_across & has_left,
        UP_LEFT: has_above2 & has_right, UP_RIGHT: has_above2 & has_left,
        DOWN_LEFT: has_below2 & has_right, DOWN_RIGHT: has_below2 & has_left,
    }
    first, second = tuple(range(6)), tuple(range(6, COPIES))

    def start(g, kinds):
        for which in kinds:
            @pl.when(sends[which])
            def _():
                copy(g, which).start()

    def arrive(g, kinds):
        for which in kinds:
            @pl.when(receives[which])
            def _():
                copy(g, which).wait_recv()

    def own_copy(g):
        return pltpu.make_async_copy(
            kv_hbm.at[g], kv_refs[g].at[:, own, slice(0, rows)], own_sems.at[g]
        )

    neighbours = (
        (has_left, {"col": col - 1}), (has_right, {"col": col + 1}),
        (has_above, {"row": row - 1}), (has_below, {"row": row + 1}),
        (has_above2, {"row": row - 2}), (has_below2, {"row": row + 2}),
    )
    barrier = pltpu.get_barrier_semaphore()
    for exists, there in neighbours:
        @pl.when(exists)
        def _():
            pl.semaphore_signal(
                barrier, inc=1, device_id=there, device_id_type=pl.DeviceIdType.MESH
            )
    for g in range(groups):
        own_copy(g).start()

    def clear(part):
        part[...] = jnp.zeros(part.shape, part.dtype)

    for g in range(groups):
        kv, extra = kv_refs[g], edge_refs[g]
        for which in range(2):
            @pl.when(jnp.logical_not(has_left))
            def _():
                clear(kv.at[which, left, : 3 * rows])
                for near in range(2):
                    clear(extra.at[which, near, edge : edge + side])

            @pl.when(jnp.logical_not(has_right))
            def _():
                clear(kv.at[which, right, : 3 * rows])
                for near in range(2):
                    clear(extra.at[which, near, edge + side :])

            @pl.when(jnp.logical_not(has_above))
            def _():
                clear(kv.at[which, :, rows : 2 * rows])

            @pl.when(jnp.logical_not(has_below))
            def _():
                clear(kv.at[which, :, 2 * rows : 3 * rows])

            @pl.when(jnp.logical_not(has_above2))
            def _():
                clear(extra.at[which, 0])

            @pl.when(jnp.logical_not(has_below2))
            def _():
                clear(extra.at[which, 1])

    pl.semaphore_wait(barrier, sum(exists.astype(jnp.int32) for exists, _ in neighbours))

    tile_lanes = 4 * rows
    low_half = lax.broadcasted_iota(jnp.int32, (rows, 2 * tile_lanes), 1) < tile_lanes
    lane_head = (
        lax.broadcasted_iota(jnp.int32, (QUERY_COLS * rows, GROUP_FEATURES), 1) // HEAD_DIM
    )

    def build_bias(g):
        step = step_ref[...]
        masked = jnp.full(step.shape, MASKED, jnp.float32)

        def one(n, carry):
            h, x = n // BIAS_STEPS, n % BIAS_STEPS
            entry = (g * GROUP + h) * WINDOW * TABLE_STEPS + x
            tile = masked
            for a in range(WINDOW):
                value = jnp.where(
                    low_half,
                    bias_ref[entry + a * TABLE_STEPS],
                    bias_ref[entry + a * TABLE_STEPS + 1],
                )
                tile = jnp.where(step == a, value, tile)
            tile_ref[0, n] = tile
            tile_ref[1, n] = jnp.where(low_half, tile, masked)
            tile_ref[2, n] = jnp.where(low_half, masked, tile)
            tile_ref[3, n] = masked
            return carry

        lax.fori_loop(0, GROUP * BIAS_STEPS, one, 0)

    def unpack_edges(g):
        spread = spread_ref[...]
        for which in range(2):
            packed = edge_refs[g][which].reshape(-1, GROUP_FEATURES)
            wide = jnp.dot(spread, packed, preferred_element_type=jnp.float32)
            kv_refs[g][which, :, 3 * rows :, :] = wide.astype(jnp.bfloat16).reshape(
                cols + 2 * HALO, rows, GROUP_FEATURES
            )

    def attend(g):
        kv = kv_refs[g]
        features = slice(g * GROUP_FEATURES, (g + 1) * GROUP_FEATURES)

        def one(p, carry):
            at = p * ENTRY
            query = jnp.concatenate(
                [query_ref[table_ref[at + t], :, features] for t in range(QUERY_COLS)], axis=0
            )
            zero = jnp.zeros_like(query)
            stacked = jnp.concatenate(
                [jnp.where(lane_head == h, query, zero) for h in range(GROUP)], axis=0
            )
            scores = []
            per = 4
            for k in range(SLOTS // per):
                keys = jnp.concatenate(
                    [
                        kv[0, table_ref[at + QUERY_COLS + k * per + s]]
                        for s in range(per)
                    ],
                    axis=0,
                )
                score = lax.dot_general(
                    stacked, keys, (((1,), (1,)), ((), ())), preferred_element_type=jnp.float32
                )
                biases = []
                for pair in range(k * per // 2, (k + 1) * per // 2):
                    kind = table_ref[at + QUERY_COLS + SLOTS + pair]
                    biases.append(
                        jnp.concatenate(
                            [
                                tile_ref[kind, h * BIAS_STEPS + 2 * pair - t + QUERY_COLS - 1]
                                for h in range(GROUP)
                                for t in range(QUERY_COLS)
                            ],
                            axis=0,
                        )
                    )
                scores.append(score + jnp.concatenate(biases, axis=1))
            peak = functools.reduce(jnp.maximum, scores)
            peak = jnp.max(peak, axis=1, keepdims=True)
            summed, total = None, None
            for k in range(SLOTS // per):
                weight = jnp.exp(scores[k] - peak)
                values = jnp.concatenate(
                    [
                        kv[1, table_ref[at + QUERY_COLS + k * per + s]]
                        for s in range(per)
                    ],
                    axis=0,
                )
                part = jnp.dot(
                    weight.astype(jnp.bfloat16), values, preferred_element_type=jnp.float32
                )
                summed = part if summed is None else summed + part
                total = weight if total is None else total + weight
            total = jnp.sum(total, axis=1, keepdims=True)
            summed = summed / total
            tall = QUERY_COLS * rows
            result = summed[:tall]
            for h in range(1, GROUP):
                result = jnp.where(lane_head == h, summed[h * tall : (h + 1) * tall], result)
            done_ref[pl.ds(p * QUERY_COLS, QUERY_COLS)] = result.astype(jnp.bfloat16).reshape(
                QUERY_COLS, rows, GROUP_FEATURES
            )
            return carry

        lax.fori_loop(0, block_count(cols), one, 0)

        def place(j, carry):
            out_ref[j, :, features] = done_ref[slot_ref[j]]
            return carry

        lax.fori_loop(0, cols, place, 0)

    start(0, first)
    if groups > 1:
        start(1, first)
    build_bias(0)
    arrive(0, first)
    start(0, second)
    if groups > 2:
        start(2, first)
    for g in range(groups):
        if g > 0:
            build_bias(g)
        if g + 1 < groups:
            arrive(g + 1, first)
            start(g + 1, second)
            if g + 3 < groups:
                start(g + 3, first)
        arrive(g, second)
        own_copy(g).wait()
        unpack_edges(g)
        attend(g)
    for g in range(groups):
        for which in range(COPIES):
            @pl.when(sends[which])
            def _():
                copy(g, which).wait_send()


def fused_attention(table, slots, bias, step, spread, query, kv, edges):
    groups, _, cols, rows, _ = kv.shape
    span = cols + 2 * HALO
    wide = edges.shape[3] + 2 * (-(-(HALO - rows) * HALO // 16) * 16)
    smem = pl.BlockSpec(memory_space=pltpu.SMEM)
    vmem = pl.BlockSpec(memory_space=pltpu.VMEM)
    hbm = pl.BlockSpec(memory_space=pl.ANY)
    blocks = block_count(cols)
    return pl.pallas_call(
        functools.partial(fused_kernel, groups, rows, cols),
        in_specs=[smem, smem, smem, vmem, vmem, vmem, hbm, hbm],
        out_specs=vmem,
        out_shape=jax.ShapeDtypeStruct(query.shape, jnp.bfloat16),
        scratch_shapes=[
            *[pltpu.VMEM((2, span, 4 * rows, GROUP_FEATURES), jnp.bfloat16)] * groups,
            *[pltpu.VMEM((2, 2, wide, GROUP_FEATURES), jnp.bfloat16)] * groups,
            pltpu.VMEM((4, GROUP * BIAS_STEPS, rows, 8 * rows), jnp.float32),
            pltpu.VMEM((blocks * QUERY_COLS, rows, GROUP_FEATURES), jnp.bfloat16),
            pltpu.SemaphoreType.DMA((groups, COPIES)),
            pltpu.SemaphoreType.DMA((groups, COPIES)),
            pltpu.SemaphoreType.DMA((groups,)),
        ],
        compiler_params=pltpu.CompilerParams(
            collective_id=0, has_side_effects=True, vmem_limit_bytes=60 * 1024 * 1024
        ),
        cost_estimate=pl.CostEstimate(
            flops=groups * blocks * 4 * 256 * 1024 * 256,
            bytes_accessed=kv.size * 8,
            transcendentals=groups * blocks * 256 * 1024,
        ),
    )(table, slots, bias, step, spread, query, kv, edges)


def block_tables(dilation, rows, cols):
    total_cols = cols * lax.axis_size("col")
    anchor = lax.axis_index("col") * cols
    span = cols + 2 * HALO
    per_class = -(-(-(-cols // dilation)) // QUERY_COLS)
    block = jnp.arange(block_count(cols), dtype=jnp.int32)
    base = block // per_class + (block % per_class) * QUERY_COLS * dilation
    base = base[:, None]
    query_cols = jnp.clip(
        base + jnp.arange(QUERY_COLS, dtype=jnp.int32)[None] * dilation, 0, cols - 1
    )
    key_cols = base + (jnp.arange(SLOTS, dtype=jnp.int32)[None] - RADIUS_MAX) * dilation
    real = (key_cols + anchor >= 0) & (key_cols + anchor < total_cols)
    low, high = real[:, 0::2], real[:, 1::2]
    kind = jnp.where(low, jnp.where(high, 0, 1), jnp.where(high, 2, 3))
    key_cols = jnp.clip(key_cols + HALO, 0, span - 1)
    table = jnp.concatenate([query_cols, key_cols, kind], axis=1).astype(jnp.int32)
    j = jnp.arange(cols, dtype=jnp.int32)
    place = j // dilation
    slots = (j % dilation * per_class + place // QUERY_COLS) * QUERY_COLS + place % QUERY_COLS
    return table.reshape(-1), slots.astype(jnp.int32)


def bias_tables(rel_bias, pattern, radius, dilation, rows):
    total_rows = rows * lax.axis_size("row")
    anchor = lax.axis_index("row") * rows
    steps = jnp.arange(WINDOW, dtype=jnp.int32) - RADIUS_MAX
    chosen = (pattern == 1) | ((steps[:, None] == 0) & (steps[None, :] == 0))
    chosen = chosen & (jnp.abs(steps)[:, None] <= radius) & (jnp.abs(steps)[None, :] <= radius)
    bias = jnp.where(chosen[None], rel_bias, MASKED)
    before = QUERY_COLS - 1
    bias = jnp.pad(
        bias, ((0, 0), (0, 0), (before, TABLE_STEPS - WINDOW - before)), constant_values=MASKED
    )
    spill = HALO - rows
    i = lax.broadcasted_iota(jnp.int32, (rows, 8 * rows), 0)
    spot = lax.broadcasted_iota(jnp.int32, (rows, 8 * rows), 1) % (4 * rows)
    extra = spot - 3 * rows
    offset = jnp.where(
        spot < rows,
        spot,
        jnp.where(
            spot < 2 * rows,
            spot - 2 * rows,
            jnp.where(
                spot < 3 * rows,
                spot - rows,
                jnp.where(extra < spill, extra - HALO, extra - spill + 2 * rows),
            ),
        ),
    )
    real = (extra < 2 * spill) & (offset + anchor >= 0) & (offset + anchor < total_rows)
    far = offset - i
    hit = real & (far % dilation == 0) & (jnp.abs(far) <= RADIUS_MAX * dilation)
    step = jnp.where(hit, far // dilation + RADIUS_MAX, -1)
    return bias.reshape(-1), step.astype(jnp.int32)


def edge_spread(rows, cols):
    spill = HALO - rows
    span = cols + 2 * HALO
    edge = spill * cols
    side = -(-spill * HALO // 16) * 16
    wide = edge + 2 * side
    kept = side // spill
    target = lax.broadcasted_iota(jnp.int32, (span * rows, 2 * wide), 0)
    packed = lax.broadcasted_iota(jnp.int32, (span * rows, 2 * wide), 1)
    at, extra = target // rows, target % rows
    near, place = packed // wide, packed % wide
    column, line = place // spill, place % spill
    column = jnp.where(
        place < edge,
        column + HALO,
        jnp.where(
            place < edge + side,
            column - cols + HALO - kept,
            column - cols - kept + HALO + cols,
        ),
    )
    hit = (at == column) & (extra == near * spill + line)
    return hit.astype(jnp.bfloat16)


def shards(
    query_map, key_map, value_map, window_mask, tile_radius, dilation_per_tile, rel_bias, out_weight
):
    rows, cols, features = query_map.shape
    groups = features // GROUP_FEATURES
    spill = HALO - rows
    dilation = dilation_per_tile[0, 0]
    table, slots = block_tables(dilation, rows, cols)
    bias, step = bias_tables(rel_bias, window_mask[0, 0], tile_radius[0, 0], dilation, rows)

    pair = jnp.stack([key_map, value_map]).reshape(2, rows, cols, groups, GROUP_FEATURES)
    kv = pair.transpose(3, 0, 2, 1, 4)
    ends = jnp.stack([pair[:, :spill], pair[:, rows - spill :]])
    edges = ends.transpose(4, 1, 0, 3, 2, 5).reshape(
        groups, 2, 2, cols * spill, GROUP_FEATURES
    )
    query = query_map.transpose(1, 0, 2) * jnp.bfloat16(1.0 / math.sqrt(HEAD_DIM))
    attended = fused_attention(
        table, slots, bias, step, edge_spread(rows, cols), query, kv, edges
    ).reshape(cols * rows, features)

    count = lax.axis_size("head")
    model = out_weight.shape[1]
    if count != 2:
        partials = jnp.dot(attended, out_weight, preferred_element_type=jnp.float32)
        mixed = lax.psum_scatter(partials, "head", scatter_dimension=1, tiled=True)
        mixed = mixed.astype(jnp.bfloat16).reshape(cols, rows, model // count)
        return mixed.transpose(1, 0, 2)
    me = lax.axis_index("head")
    half = model // 2
    theirs = lax.dynamic_slice_in_dim(out_weight, (1 - me) * half, half, 1)
    mine = lax.dynamic_slice_in_dim(out_weight, me * half, half, 1)
    mixed = []
    parts = 2
    tokens = rows * cols // parts
    for part in range(parts):
        block = attended[part * tokens : (part + 1) * tokens]
        sent = jnp.dot(block, theirs, preferred_element_type=jnp.float32).astype(jnp.bfloat16)
        got = lax.ppermute(sent, "head", [(0, 1), (1, 0)])
        kept = jnp.dot(block, mine, preferred_element_type=jnp.float32)
        mixed.append((kept + got.astype(jnp.float32)).astype(jnp.bfloat16))
    return jnp.concatenate(mixed).reshape(cols, rows, half).transpose(1, 0, 2)


def solution(mesh):
    placed = (
        P("row", "col", "head"),
        P("row", "col", "head"),
        P("row", "col", "head"),
        P("row", "col", None, None),
        P("row", "col"),
        P("row", "col"),
        P("head", None, None),
        P("head", None),
    )
    return jax.shard_map(
        shards, mesh=mesh, in_specs=placed, out_specs=P("row", "col", "head"), check_vma=False
    )
```

time: 252 us -> 168 us (0.67)
  the two profiles are of different devices: /device:TPU:0 before, /device:TPU:1 now
where the time goes in v1:
time: 168 us
  Pallas kernels  98.3 us (59%)
  waiting for transfers between devices  21.7 us (13%)
  local copies, waits for them, and re-layouts  20.1 us (12%)
  matrix products  16.7 us (10%)
  other arithmetic  7.8 us (5%)
    pallas_call x1, Pallas kernels, fused_attention(): pl.pallas_call(functools.partial(fused_kernel, groups, rows, cols), in_sp...  98.3 us
    ppermute x2, waiting for transfers between devices, shards(): got = lax.ppermute(sent, 'head', [(0, 1), (1, 0)])  21.7 us
    dot_general x2, matrix products, shards(): jnp.dot(block, theirs, preferred_element_type=jnp.float32)  9.23 us
    another operation x3, local copies, waits for them, and re-layouts, shards(): jnp.stack([key_map, value_map])  8.68 us
    dot_general x2, matrix products, shards(): kept = jnp.dot(block, mine, preferred_element_type=jnp.float32)  7.43 us
  transfers between devices with their start and end apart: 2, of which 2 were waited for; matrix products, arithmetic and copies ran while one was open for 5% of the time, Pallas kernels for 0%

profile of v1, /device:TPU:1, one launch (start us, length us, event | category | flops | bytes accessed | tf_op | source)
XLA Modules:
  0.0 167.6 jit_solution(5753925549148239636)
XLA Ops:
  0.7 0.1 multiply_add_fusion
  0.9 0.1 fusion.41
  0.9 0.1 slice.24
  1.0 0.1 slice.25
  1.2 0.1 fusion.32
  1.3 0.1 add_clamp_fusion
  1.4 0.1 pad_add_fusion
  1.5 0.6 reshape.140.table_ref
  2.1 3.3 %stack.18 = bf16[1,16,32,6,256]{4,3,2,1,0:T(8,128)(2,1)S(1)} reshape(bf16[16,32,1536]{2,1,0:T(8,128)(2,1)} %param.9) | data formatting | bytes 3145728 | tf_op jit(solution)/shard_map/stack | solution.py:454
  5.5 2.0 %copy_dynamic-update-slice_fusion.1 = bf16[2,16,32,6,256]{4,1,2,0,3:T(8,128)(2,1)} fusion(bf16[1,16,32,6,256]{4,3,2,1,0:T(8,128)(2,1)S(1)} %stack.18), kind=kLoop, calls=%fused_computation.32 | loop fusion | bytes 3145728
  7.5 3.3 %stack.19 = bf16[1,16,32,6,256]{4,3,2,1,0:T(8,128)(2,1)S(1)} reshape(bf16[16,32,1536]{2,1,0:T(8,128)(2,1)} %param.10) | data formatting | bytes 3145728 | tf_op jit(solution)/shard_map/stack | solution.py:454
  10.8 2.1 %copy_dynamic-update-slice_fusion = bf16[2,16,32,6,256]{4,1,2,0,3:T(8,128)(2,1)} fusion(bf16[2,16,32,6,256]{4,1,2,0,3:T(8,128)(2,1)} %copy_dynamic-update-slice_fusion.1, bf16[1,16,32,6,256]{4,3,2,1,0:T(8,128)(2,1)S(1)} %stack.19), kind=kLoop, calls=%fused_computation.31 | loop fusion | bytes 3145728 | tf_op jit(solution)/shard_map/stack | solution.py:454
  12.9 2.7 %slice_bitcast_fusion.1 = (bf16[1,2,2,32,6,256]{5,2,3,1,4,0:T(2,128)(2,1)S(1)}, bf16[1,2,2,32,6,256]{5,2,3,1,4,0:T(2,128)(2,1)S(1)}) fusion(bf16[2,16,32,6,256]{4,1,2,0,3:T(8,128)(2,1)} %copy_dynamic-update-slice_fusion), kind=kLoop, calls=%fused_computation.39 | loop fusion | bytes 1572864 | tf_op jit(solution)/shard_map/stack | solution.py:456
  15.6 1.1 maximum_bitcast_fusion
  16.7 0.0 copy-start.2
  16.7 0.0 copy-start.1
  16.7 0.3 reshape.144
  17.0 0.0 copy-start
  17.0 0.9 copy.18.edge_hbm
  18.6 0.0 copy-done.2
  18.7 0.1 fusion.47
  18.7 0.0 copy-done.1
  18.7 0.1 broadcast_select_fusion
  18.9 0.2 copy.20
  19.0 0.1 pad.4.clone
  19.1 0.8 reshape.141.bias_ref
  19.9 0.0 copy-done
  20.0 2.1 %fusion.22.query_ref = bf16[32,16,1536]{2,1,0:T(8,128)(2,1)} fusion(bf16[16,32,1536]{2,1,0:T(8,128)(2,1)S(1)} %copy-done), kind=kLoop, calls=%fused_computation.34 | loop fusion | flops 786432 | bytes 3145728 | tf_op jit(solution)/shard_map/mul | solution.py:460
  22.1 0.6 fusion.55.slot_ref
  22.7 0.8 fusion.35.step_ref
  23.5 2.3 %fusion.21.spread_ref = bf16[1088,320]{1,0:T(8,128)(2,1)} fusion(s32[320]{0:T(512)S(1)} %get-tuple-element.19, s32[320]{0:T(512)S(1)} %get-tuple-element.22, s32[1088]{0:T(1024)S(1)} %get-tuple-element.14, s32[1088]{0:T(1024)S(1)} %get-tuple-element.15, s32[320]{0:T(512)S(1)} %get-tuple-element.20, s32[320]{0:T(512)S(1)} %get-tuple-element.21, ...), kind=kLoop, calls=%fused_computation.28 | loop fusion | flops 12533760 | bytes 721664 | tf_op jit(solution)/shard_map/convert_element_type | solution.py:441
  25.8 98.3 %shard_map.82 = bf16[32,16,1536]{2,1,0:T(8,128)(2,1)} custom-call(s32[252]{0:T(256)} %reshape.140.table_ref, s32[32]{0:T(128)} %fusion.55.slot_ref, f32[5928]{0:T(1024)} %reshape.141.bias_ref, s32[16,128]{1,0:T(8,128)} %fusion.35.step_ref, bf16[1088,320]{1,0:T(8,128)(2,1)} %fusion.21.spread_ref, bf16[32,16,1536]{2,1,0:T(8,128)(2,1)} %fusion.22.query_ref, ...), custom_call_target="tpu_custom_call" | custom-call | flops 14495514624 | bytes 12582912 | tf_op jit(solution)/shard_map/pallas_call | solution.py:336
  124.2 1.5 fusion.65
  125.7 4.6 %fusion.8 = bf16[256,1536]{1,0:T(8,128)(2,1)} fusion(bf16[256,1536]{1,0:T(8,128)(2,1)S(1)} %bitcast.45, bf16[1536,3072]{1,0:T(8,128)(2,1)} %param.15, s32[]{:T(128)S(6)} %select_n.221), kind=kOutput, calls=%fused_computation.14 | convolution fusion | flops 1208352768 | bytes 6291460 | tf_op jit(solution)/shard_map/dot_general | solution.py:481
  130.3 1.2 collective-permute-start
  131.6 4.6 %fusion.11 = bf16[256,1536]{1,0:T(8,128)(2,1)} fusion(bf16[256,1536]{1,0:T(8,128)(2,1)S(1)} %bitcast.43, bf16[1536,3072]{1,0:T(8,128)(2,1)} %param.15, s32[]{:T(128)S(6)} %select_n.221), kind=kOutput, calls=%fused_computation.15 | convolution fusion | flops 1208352768 | bytes 6291460 | tf_op jit(solution)/shard_map/dot_general | solution.py:481
  136.1 0.2 collective-permute-start.1
  136.4 13.7 %collective-permute-done = bf16[256,1536]{1,0:T(8,128)(2,1)S(1)} collective-permute-done((bf16[256,1536]{1,0:T(8,128)(2,1)}, bf16[256,1536]{1,0:T(8,128)(2,1)S(1)}, u32[]{:S(2)}, u32[]{:S(2)}) %collective-permute-start) | collective-permute-done | bytes 786464 | tf_op jit(solution)/shard_map/ppermute | solution.py:482
  150.1 3.7 %add_convert_fusion.1 = bf16[256,1536]{1,0:T(8,128)(2,1)S(1)} fusion(bf16[256,1536]{1,0:T(8,128)(2,1)S(1)} %collective-permute-done, bf16[256,1536]{1,0:T(8,128)(2,1)S(1)} %bitcast.46, bf16[1536,3072]{1,0:T(8,128)(2,1)} %param.15, s32[]{:T(128)S(6)} %select_n.220), kind=kOutput, calls=%fused_computation.36 | convolution fusion | flops 1209139200 | bytes 7077892 | tf_op jit(solution)/shard_map/dot_general | solution.py:483
  153.8 8.0 %collective-permute-done.1 = bf16[256,1536]{1,0:T(8,128)(2,1)S(1)} collective-permute-done((bf16[256,1536]{1,0:T(8,128)(2,1)}, bf16[256,1536]{1,0:T(8,128)(2,1)S(1)}, u32[]{:S(2)}, u32[]{:S(2)}) %collective-permute-start.1) | collective-permute-done | bytes 786464 | tf_op jit(solution)/shard_map/ppermute | solution.py:482
  161.8 3.7 %add_convert_fusion = bf16[256,1536]{1,0:T(8,128)(2,1)S(1)} fusion(bf16[256,1536]{1,0:T(8,128)(2,1)S(1)} %collective-permute-done.1, bf16[256,1536]{1,0:T(8,128)(2,1)S(1)} %bitcast.44, bf16[1536,3072]{1,0:T(8,128)(2,1)} %param.15, s32[]{:T(128)S(6)} %select_n.220), kind=kOutput, calls=%fused_computation.35 | convolution fusion | flops 1209139200 | bytes 7077892 | tf_op jit(solution)/shard_map/dot_general | solution.py:483
  165.5 0.1 pad_maximum_fusion
  165.6 2.0 %copy.28 = bf16[32,16,1536]{2,0,1:T(8,128)(2,1)} copy(bf16[32,16,1536]{2,1,0:T(8,128)(2,1)S(1)} %bitcast.41) | data formatting | bytes 3145728 | tf_op jit(solution)/shard_map/reshape | solution.py:485
  (13 shorter events, 0.1 us)
Async XLA Ops:
  16.7 2.0 %copy-start.2 = (s32[1,1,13,13]{3,1,2,0:T(1,128)S(1)}, s32[1,1,13,13]{3,1,2,0:T(1,128)}, u32[]{:S(2)}) copy-start(s32[1,1,13,13]{3,1,2,0:T(1,128)} %param.11) | copy-start | bytes 2032
  16.7 2.1 %copy-start.1 = (f32[24,13,13]{0,2,1:T(8,128)S(1)}, f32[24,13,13]{0,2,1:T(8,128)}, u32[]{:S(2)}) copy-start(f32[24,13,13]{0,2,1:T(8,128)} %param.14) | copy-start | bytes 48676
  17.0 2.9 %copy-start = (bf16[16,32,1536]{2,1,0:T(8,128)(2,1)S(1)}, bf16[16,32,1536]{2,1,0:T(8,128)(2,1)}, u32[]{:S(2)}) copy-start(bf16[16,32,1536]{2,1,0:T(8,128)(2,1)} %param.8) | copy-start | bytes 4718596
  130.3 19.8 %collective-permute-start = (bf16[256,1536]{1,0:T(8,128)(2,1)}, bf16[256,1536]{1,0:T(8,128)(2,1)S(1)}, u32[]{:S(2)}, u32[]{:S(2)}) collective-permute-start(bf16[256,1536]{1,0:T(8,128)(2,1)} %fusion.8), channel_id=1, source_target_pairs={{0,1},{1,0},{2,3},{3,2},{4,5},{5,4},{6,7},{7,6},{8,9},{9,8},{10,11... | collective-permute-start | bytes 2359304 | tf_op jit(solution)/shard_map/ppermute | solution.py:482
  136.1 25.6 %collective-permute-start.1 = (bf16[256,1536]{1,0:T(8,128)(2,1)}, bf16[256,1536]{1,0:T(8,128)(2,1)S(1)}, u32[]{:S(2)}, u32[]{:S(2)}) collective-permute-start(bf16[256,1536]{1,0:T(8,128)(2,1)} %fusion.11), channel_id=1, source_target_pairs={{0,1},{1,0},{2,3},{3,2},{4,5},{5,4},{6,7},{7,6},{8,9},{9,8},{10,11... | collective-permute-start | bytes 2359304 | tf_op jit(solution)/shard_map/ppermute | solution.py:482

commit v2 on v1

--- a/solution.py
+++ b/solution.py
@@ -28,6 +28,10 @@
 MATE_LEFT, MATE_RIGHT, ACROSS_LEFT, ACROSS_RIGHT = range(6, 10)
 UP_LEFT, UP_RIGHT, DOWN_LEFT, DOWN_RIGHT = range(10, 14)
 COPIES = 14
+SWAP, SWAP_MATE, SWAP_ACROSS, SWAP_LAST = range(4)
+SWAPS = 4
+TILE_KEYS = 256
+LEAD, TRAIL = 2, 2
 
 
 def block_count(cols):
@@ -37,11 +41,16 @@
 
 
 def fused_kernel(
-    groups, rows, cols, table_ref, slot_ref, bias_ref, step_ref, spread_ref, query_ref,
-    kv_hbm, edge_hbm, out_ref, *scratch
+    groups, rows, cols, table_ref, bias_ref, step_ref, slot_ref, query_ref, key_ref, value_ref,
+    weight_hbm, out_ref, *scratch
 ):
     kv_refs, edge_refs = scratch[:groups], scratch[groups : 2 * groups]
-    tile_ref, done_ref, send_sems, recv_sems, own_sems = scratch[2 * groups :]
+    (
+        end_ref, tile_ref, score_a, score_b, weight_a, weight_b, total_a, total_b, turned_ref,
+        done_ref, swap_ref, place_ref, spread_ref, own_ref, other_ref, mine_ref, theirs_ref,
+        sum_ref, send_sems, recv_sems, swap_send, swap_recv, head_send, head_recv, own_sem,
+    ) = scratch[2 * groups :]
+    score_refs, weight_refs, total_refs = (score_a, score_b), (weight_a, weight_b), (total_a, total_b)
     spill = HALO - rows
     own = slice(HALO, HALO + cols)
     left, right = slice(0, HALO), slice(HALO + cols, cols + 2 * HALO)
@@ -65,12 +74,12 @@
         up, down = slice(rows, 2 * rows), slice(2 * rows, 3 * rows)
         near_left, near_right = slice(HALO, 2 * HALO), slice(cols, cols + HALO)
         source, target, there = {
-            TO_LEFT: (kv_hbm.at[g, :, :HALO], kv.at[:, right, base], {"col": col - 1}),
-            TO_RIGHT: (kv_hbm.at[g, :, cols - HALO :], kv.at[:, left, base], {"col": col + 1}),
-            TO_ABOVE: (kv_hbm.at[g], kv.at[:, own, down], {"row": row - 1}),
-            TO_BELOW: (kv_hbm.at[g], kv.at[:, own, up], {"row": row + 1}),
-            TOP_UP: (edge_hbm.at[g, :, 0], extra.at[:, 1, :edge], {"row": row - 2}),
-            BOTTOM_DOWN: (edge_hbm.at[g, :, 1], extra.at[:, 0, :edge], {"row": row + 2}),
+            TO_LEFT: (kv.at[:, near_left, base], kv.at[:, right, base], {"col": col - 1}),
+            TO_RIGHT: (kv.at[:, near_right, base], kv.at[:, left, base], {"col": col + 1}),
+            TO_ABOVE: (kv.at[:, own, base], kv.at[:, own, down], {"row": row - 1}),
+            TO_BELOW: (kv.at[:, own, base], kv.at[:, own, up], {"row": row + 1}),
+            TOP_UP: (end_ref.at[g, :, 0], extra.at[:, 1, :edge], {"row": row - 2}),
+            BOTTOM_DOWN: (end_ref.at[g, :, 1], extra.at[:, 0, :edge], {"row": row + 2}),
             MATE_LEFT: (kv.at[:, left, base], kv.at[:, left, mate_rows], {"row": mate}),
             MATE_RIGHT: (kv.at[:, right, base], kv.at[:, right, mate_rows], {"row": mate}),
             ACROSS_LEFT: (
@@ -128,15 +137,42 @@
             def _():
                 copy(g, which).wait_recv()
 
-    def own_copy(g):
-        return pltpu.make_async_copy(
-            kv_hbm.at[g], kv_refs[g].at[:, own, slice(0, rows)], own_sems.at[g]
+    head = lax.axis_index("head")
+    half = out_ref.shape[1]
+    quarter = theirs_ref.shape[0] // 4
+    paired = row + 2 - 4 * lax.rem(row // 2, 2)
+    mine = pl.ds(pl.multiple_of(lax.rem(row, 4) * quarter, quarter), quarter)
+    passed = pl.ds(pl.multiple_of(lax.rem(paired, 4) * quarter, quarter), quarter)
+    there_cols = pl.ds(pl.multiple_of((1 - head) * half, half), half)
+    own_weight = pltpu.make_async_copy(
+        weight_hbm.at[:, pl.ds(pl.multiple_of(head * half, half), half)], mine_ref, own_sem
+    )
+
+    def swap_copy(which):
+        source, target, there = {
+            SWAP: (weight_hbm.at[mine, there_cols], theirs_ref.at[mine], {"head": 1 - head}),
+            SWAP_MATE: (theirs_ref.at[mine], theirs_ref.at[mine], {"row": mate}),
+            SWAP_ACROSS: (theirs_ref.at[mine], theirs_ref.at[mine], {"row": paired}),
+            SWAP_LAST: (theirs_ref.at[passed], theirs_ref.at[passed], {"row": mate}),
+        }[which]
+        return pltpu.make_async_remote_copy(
+            src_ref=source, dst_ref=target, send_sem=swap_send.at[which],
+            recv_sem=swap_recv.at[which], device_id=there,
+            device_id_type=pl.DeviceIdType.MESH,
+        )
+
+    def head_copy(g):
+        return pltpu.make_async_remote_copy(
+            src_ref=own_ref.at[g], dst_ref=other_ref.at[g], send_sem=head_send.at[g],
+            recv_sem=head_recv.at[g], device_id={"head": 1 - head},
+            device_id_type=pl.DeviceIdType.MESH,
         )
 
     neighbours = (
         (has_left, {"col": col - 1}), (has_right, {"col": col + 1}),
         (has_above, {"row": row - 1}), (has_below, {"row": row + 1}),
         (has_above2, {"row": row - 2}), (has_below2, {"row": row + 2}),
+        (head >= 0, {"head": 1 - head}),
     )
     barrier = pltpu.get_barrier_semaphore()
     for exists, there in neighbours:
@@ -145,8 +181,7 @@
             pl.semaphore_signal(
                 barrier, inc=1, device_id=there, device_id_type=pl.DeviceIdType.MESH
             )
-    for g in range(groups):
-        own_copy(g).start()
+    own_weight.start()
 
     def clear(part):
         part[...] = jnp.zeros(part.shape, part.dtype)
@@ -182,6 +217,33 @@
             def _():
                 clear(extra.at[which, 1])
 
+    def iota(shape, axis):
+        return lax.broadcasted_iota(jnp.int32, shape, axis)
+
+    tokens = rows * cols
+    place, source = iota((tokens, tokens), 0), iota((tokens, tokens), 1)
+    swap_ref[:tokens] = (source == place % rows * cols + place // rows).astype(
+        jnp.float32
+    ).astype(jnp.bfloat16)
+    place, source = iota((2 * edge, tokens), 0), iota((2 * edge, tokens), 1)
+    line = place % edge % spill + jnp.where(place < edge, 0, rows - spill)
+    swap_ref[tokens:] = (source == line * cols + place % edge // spill).astype(
+        jnp.float32
+    ).astype(jnp.bfloat16)
+
+    def turn(g):
+        features = slice(g * GROUP_FEATURES, (g + 1) * GROUP_FEATURES)
+        for which, ref in ((0, key_ref), (1, value_ref)):
+            moved = jnp.dot(
+                swap_ref[...], ref[:, :, features].reshape(-1, GROUP_FEATURES),
+                preferred_element_type=jnp.float32,
+            ).astype(jnp.bfloat16)
+            kv_refs[g][which, own, :rows] = moved[:tokens].reshape(cols, rows, GROUP_FEATURES)
+            end_ref[g, which] = moved[tokens:].reshape(2, edge, GROUP_FEATURES)
+
+    turn(0)
+    if groups > 1:
+        turn(1)
     pl.semaphore_wait(barrier, sum(exists.astype(jnp.int32) for exists, _ in neighbours))
 
     tile_lanes = 4 * rows
@@ -225,137 +287,246 @@
     def attend(g):
         kv = kv_refs[g]
         features = slice(g * GROUP_FEATURES, (g + 1) * GROUP_FEATURES)
-
-        def one(p, carry):
-            at = p * ENTRY
+        near = TILE_KEYS // (4 * rows)
+        tall = QUERY_COLS * rows
+        blocks = block_count(cols)
+        turned = jnp.dot(
+            swap_ref[: rows * cols], query_ref[:, :, features].reshape(-1, GROUP_FEATURES),
+            preferred_element_type=jnp.float32,
+        ) * (1.0 / math.sqrt(HEAD_DIM))
+        turned_ref[...] = turned.astype(jnp.bfloat16).reshape(cols, rows, GROUP_FEATURES)
+
+        def keys_at(p, which, k):
+            at = p * ENTRY + QUERY_COLS + k * near
+            return jnp.concatenate(
+                [kv[which, table_ref[at + s]] for s in range(near)], axis=0
+            )
+
+        def multiply(p, score_ref):
             query = jnp.concatenate(
-                [query_ref[table_ref[at + t], :, features] for t in range(QUERY_COLS)], axis=0
+                [turned_ref[table_ref[p * ENTRY + t]] for t in range(QUERY_COLS)], axis=0
             )
             zero = jnp.zeros_like(query)
             stacked = jnp.concatenate(
                 [jnp.where(lane_head == h, query, zero) for h in range(GROUP)], axis=0
             )
-            scores = []
-            per = 4
-            for k in range(SLOTS // per):
-                keys = jnp.concatenate(
-                    [
-                        kv[0, table_ref[at + QUERY_COLS + k * per + s]]
-                        for s in range(per)
-                    ],
-                    axis=0,
+            for k in range(SLOTS // near):
+                score_ref[:, k * TILE_KEYS : (k + 1) * TILE_KEYS] = lax.dot_general(
+                    stacked, keys_at(p, 0, k), (((1,), (1,)), ((), ())),
+                    preferred_element_type=jnp.float32,
                 )
-                score = lax.dot_general(
-                    stacked, keys, (((1,), (1,)), ((), ())), preferred_element_type=jnp.float32
+
+        def soften(p, score_ref, weight_ref, total_ref):
+            at = p * ENTRY + QUERY_COLS + SLOTS
+            kinds = [table_ref[at + pair] for pair in range(PAIRS)]
+            lanes = 8 * rows
+            for h in range(GROUP):
+                for t in range(QUERY_COLS):
+                    here = slice((h * QUERY_COLS + t) * rows, (h * QUERY_COLS + t + 1) * rows)
+                    parts = [
+                        score_ref[here, pair * lanes : (pair + 1) * lanes]
+                        + tile_ref[kinds[pair], h * BIAS_STEPS + 2 * pair - t + QUERY_COLS - 1]
+                        for pair in range(PAIRS)
+                    ]
+                    peak = jnp.max(functools.reduce(jnp.maximum, parts), axis=1, keepdims=True)
+                    parts = [jnp.exp(part - peak) for part in parts]
+                    total = jnp.sum(functools.reduce(jnp.add, parts), axis=1, keepdims=True)
+                    for pair in range(PAIRS):
+                        weight_ref[here, pair * lanes : (pair + 1) * lanes] = parts[pair].astype(
+                            jnp.bfloat16
+                        )
+                    total_ref[here] = jnp.broadcast_to(total, (rows, GROUP_FEATURES // 2))
+
+        def finish(p, weight_ref, total_ref):
+            values = jnp.concatenate(
+                [keys_at(p, 1, k) for k in range(SLOTS // near)], axis=0
+            )
+            summed = jnp.dot(weight_ref[...], values, preferred_element_type=jnp.float32)
+            result = summed[:tall]
+            total = total_ref[...]
+            total = jnp.concatenate([total, total], axis=1)
+            share = total[:tall]
+            for h in range(1, GROUP):
+                part = slice(h * tall, (h + 1) * tall)
+                result = jnp.where(lane_head == h, summed[part], result)
+                share = jnp.where(lane_head == h, total[part], share)
+            row_at = p * tall if isinstance(p, int) else pl.multiple_of(p * tall, tall)
+            done_ref[pl.ds(row_at, tall)] = (result / share).astype(
+                jnp.bfloat16
+            )
+
+        def two(n, carry):
+            for side in range(2):
+                i = 2 * n + side
+                finish(i, weight_refs[side], total_refs[side])
+                soften(
+                    i + 1, score_refs[1 - side], weight_refs[1 - side], total_refs[1 - side]
                 )
-                biases = []
-                for pair in range(k * per // 2, (k + 1) * per // 2):
-                    kind = table_ref[at + QUERY_COLS + SLOTS + pair]
-                    biases.append(
-                        jnp.concatenate(
-                            [
-                                tile_ref[kind, h * BIAS_STEPS + 2 * pair - t + QUERY_COLS - 1]
-                                for h in range(GROUP)
-                                for t in range(QUERY_COLS)
-                            ],
-                            axis=0,
-                        )
-                    )
-                scores.append(score + jnp.concatenate(biases, axis=1))
-            peak = functools.reduce(jnp.maximum, scores)
-            peak = jnp.max(peak, axis=1, keepdims=True)
-            summed, total = None, None
-            for k in range(SLOTS // per):
-                weight = jnp.exp(scores[k] - peak)
-                values = jnp.concatenate(
-                    [
-                        kv[1, table_ref[at + QUERY_COLS + k * per + s]]
-                        for s in range(per)
-                    ],
-                    axis=0,
-                )
-                part = jnp.dot(
-                    weight.astype(jnp.bfloat16), values, preferred_element_type=jnp.float32
-                )
-                summed = part if summed is None else summed + part
-                total = weight if total is None else total + weight
-            total = jnp.sum(total, axis=1, keepdims=True)
-            summed = summed / total
-            tall = QUERY_COLS * rows
-            result = summed[:tall]
-            for h in range(1, GROUP):
-                result = jnp.where(lane_head == h, summed[h * tall : (h + 1) * tall], result)
-            done_ref[pl.ds(p * QUERY_COLS, QUERY_COLS)] = result.astype(jnp.bfloat16).reshape(
-                QUERY_COLS, rows, GROUP_FEATURES
-            )
+                multiply(i + 2, score_refs[side])
             return carry
 
-        lax.fori_loop(0, block_count(cols), one, 0)
-
-        def place(j, carry):
-            out_ref[j, :, features] = done_ref[slot_ref[j]]
-            return carry
-
-        lax.fori_loop(0, cols, place, 0)
+        steps = blocks + 1
+        lax.fori_loop(0, -(-steps // 2), two, 0)
+        if steps % 2 == 0:
+            finish(LEAD + blocks - 1, weight_refs[(blocks - 1) % 2], total_refs[(blocks - 1) % 2])
+
+        own_ref[g] = jnp.dot(
+            place_ref[...], done_ref[LEAD * tall :], preferred_element_type=jnp.float32
+        ).astype(jnp.bfloat16)
 
     start(0, first)
+    swap_copy(SWAP).start()
     if groups > 1:
         start(1, first)
+    span = cols + 2 * HALO
+    wide = spread_ref.shape[1] // 2
+    kept = side // spill
+    target, packed = iota(spread_ref.shape, 0), iota(spread_ref.shape, 1)
+    at, line = target // rows, target % rows
+    second_half = packed >= wide
+    spot = packed - jnp.where(second_half, wide, 0)
+    column = spot // spill
+    column = jnp.where(
+        spot < edge,
+        column + HALO,
+        jnp.where(spot < edge + side, column - cols + HALO - kept, column - kept + HALO),
+    )
+    wanted = jnp.where(second_half, spill, 0) + spot % spill
+    spread_ref[...] = ((at == column) & (line == wanted)).astype(jnp.float32).astype(jnp.bfloat16)
+    place_ref[...] = (
+        iota(place_ref.shape, 1) == jnp.broadcast_to(slot_ref[...], place_ref.shape)
+    ).astype(jnp.float32).astype(jnp.bfloat16)
+    for g in range(2, groups):
+        turn(g)
     build_bias(0)
     arrive(0, first)
     start(0, second)
     if groups > 2:
         start(2, first)
+
+    model_tiles = half // GROUP_FEATURES
+
+    def project(g):
+        weights = slice(g * GROUP_FEATURES, (g + 1) * GROUP_FEATURES)
+
+        def one(n, carry):
+            lanes = pl.ds(pl.multiple_of(n * GROUP_FEATURES, GROUP_FEATURES), GROUP_FEATURES)
+            part = jnp.dot(own_ref[g], mine_ref[weights, lanes], preferred_element_type=jnp.float32)
+            sum_ref[:, lanes] = part if g == 0 else sum_ref[:, lanes] + part
+            return carry
+
+        lax.fori_loop(0, model_tiles, one, 0)
+
+    pass_on, pass_last = min(2, groups - 1), min(4, groups - 1)
     for g in range(groups):
         if g > 0:
+            head_copy(g - 1).start()
             build_bias(g)
         if g + 1 < groups:
             arrive(g + 1, first)
             start(g + 1, second)
             if g + 3 < groups:
                 start(g + 3, first)
+        if g == pass_on:
+            swap_copy(SWAP).wait_recv()
+            swap_copy(SWAP_ACROSS).start()
+            swap_copy(SWAP_MATE).start()
+        if g == pass_last:
+            swap_copy(SWAP_ACROSS).wait_recv()
+            swap_copy(SWAP_LAST).start()
         arrive(g, second)
-        own_copy(g).wait()
         unpack_edges(g)
         attend(g)
+        if g == 0:
+            own_weight.wait()
+        project(g)
+    head_copy(groups - 1).start()
+    swap_copy(SWAP_MATE).wait_recv()
+    swap_copy(SWAP_LAST).wait_recv()
+    for g in range(groups):
+        head_copy(g).wait_recv()
+
+    def last(n, carry):
+        lanes = pl.ds(pl.multiple_of(n * GROUP_FEATURES, GROUP_FEATURES), GROUP_FEATURES)
+        total = sum_ref[:, lanes]
+        for g in range(groups):
+            weights = slice(g * GROUP_FEATURES, (g + 1) * GROUP_FEATURES)
+            total = total + jnp.dot(
+                other_ref[g], theirs_ref[weights, lanes], preferred_element_type=jnp.float32
+            )
+        out_ref[:, lanes] = total.astype(jnp.bfloat16)
+        return carry
+
+    lax.fori_loop(0, model_tiles, last, 0)
     for g in range(groups):
         for which in range(COPIES):
             @pl.when(sends[which])
             def _():
                 copy(g, which).wait_send()
-
-
-def fused_attention(table, slots, bias, step, spread, query, kv, edges):
-    groups, _, cols, rows, _ = kv.shape
+        head_copy(g).wait_send()
+    for which in range(SWAPS):
+        swap_copy(which).wait_send()
+
+
+def fused_layer(table, bias, step, slots, query, key, value, weight):
+    rows, cols, features = query.shape
+    groups = features // GROUP_FEATURES
+    tokens = rows * cols
+    half = weight.shape[1] // 2
     span = cols + 2 * HALO
-    wide = edges.shape[3] + 2 * (-(-(HALO - rows) * HALO // 16) * 16)
+    spill = HALO - rows
+    edge = spill * cols
+    wide = edge + 2 * (-(-spill * HALO // 16) * 16)
     smem = pl.BlockSpec(memory_space=pltpu.SMEM)
     vmem = pl.BlockSpec(memory_space=pltpu.VMEM)
     hbm = pl.BlockSpec(memory_space=pl.ANY)
     blocks = block_count(cols)
+    stacked = GROUP * QUERY_COLS * rows
+    keys = SLOTS * 4 * rows
+    half_type = jnp.bfloat16
     return pl.pallas_call(
         functools.partial(fused_kernel, groups, rows, cols),
-        in_specs=[smem, smem, smem, vmem, vmem, vmem, hbm, hbm],
+        in_specs=[smem, smem, vmem, vmem, vmem, vmem, vmem, hbm],
         out_specs=vmem,
-        out_shape=jax.ShapeDtypeStruct(query.shape, jnp.bfloat16),
+        out_shape=jax.ShapeDtypeStruct((tokens, half), half_type),
         scratch_shapes=[
-            *[pltpu.VMEM((2, span, 4 * rows, GROUP_FEATURES), jnp.bfloat16)] * groups,
-            *[pltpu.VMEM((2, 2, wide, GROUP_FEATURES), jnp.bfloat16)] * groups,
+            *[pltpu.VMEM((2, span, 4 * rows, GROUP_FEATURES), half_type)] * groups,
+            *[pltpu.VMEM((2, 2, wide, GROUP_FEATURES), half_type)] * groups,
+            pltpu.VMEM((groups, 2, 2, edge, GROUP_FEATURES), half_type),
             pltpu.VMEM((4, GROUP * BIAS_STEPS, rows, 8 * rows), jnp.float32),
-            pltpu.VMEM((blocks * QUERY_COLS, rows, GROUP_FEATURES), jnp.bfloat16),
+            pltpu.VMEM((stacked, keys), jnp.float32),
+            pltpu.VMEM((stacked, keys), jnp.float32),
+            pltpu.VMEM((stacked, keys), half_type),
+            pltpu.VMEM((stacked, keys), half_type),
+            pltpu.VMEM((stacked, GROUP_FEATURES // 2), jnp.float32),
+            pltpu.VMEM((stacked, GROUP_FEATURES // 2), jnp.float32),
+            pltpu.VMEM((cols, rows, GROUP_FEATURES), half_type),
+            pltpu.VMEM(((LEAD + blocks) * QUERY_COLS * rows, GROUP_FEATURES), half_type),
+            pltpu.VMEM((tokens + 2 * edge, tokens), half_type),
+            pltpu.VMEM((tokens, blocks * QUERY_COLS * rows), half_type),
+            pltpu.VMEM((span * rows, 2 * wide), half_type),
+            pltpu.VMEM((groups, tokens, GROUP_FEATURES), half_type),
+            pltpu.VMEM((groups, tokens, GROUP_FEATURES), half_type),
+            pltpu.VMEM((features, half), half_type),
+            pltpu.VMEM((features, half), half_type),
+            pltpu.VMEM((tokens, half), jnp.float32),
             pltpu.SemaphoreType.DMA((groups, COPIES)),
             pltpu.SemaphoreType.DMA((groups, COPIES)),
+            pltpu.SemaphoreType.DMA((SWAPS,)),
+            pltpu.SemaphoreType.DMA((SWAPS,)),
             pltpu.SemaphoreType.DMA((groups,)),
+            pltpu.SemaphoreType.DMA((groups,)),
+            pltpu.SemaphoreType.DMA,
         ],
         compiler_params=pltpu.CompilerParams(
-            collective_id=0, has_side_effects=True, vmem_limit_bytes=60 * 1024 * 1024
+            collective_id=0, has_side_effects=True, vmem_limit_bytes=67043328
         ),
         cost_estimate=pl.CostEstimate(
-            flops=groups * blocks * 4 * 256 * 1024 * 256,
-            bytes_accessed=kv.size * 8,
-            transcendentals=groups * blocks * 256 * 1024,
+            flops=groups * blocks * 4 * stacked * keys * GROUP_FEATURES,
+            bytes_accessed=query.size * 8,
+            transcendentals=groups * blocks * stacked * keys,
         ),
-    )(table, slots, bias, step, spread, query, kv, edges)
+    )(table, bias, step, slots, query, key, value, weight)
 
 
 def block_tables(dilation, rows, cols):
@@ -375,10 +546,12 @@
     kind = jnp.where(low, jnp.where(high, 0, 1), jnp.where(high, 2, 3))
     key_cols = jnp.clip(key_cols + HALO, 0, span - 1)
     table = jnp.concatenate([query_cols, key_cols, kind], axis=1).astype(jnp.int32)
+    table = jnp.pad(table, ((LEAD, TRAIL), (0, 0)))
     j = jnp.arange(cols, dtype=jnp.int32)
     place = j // dilation
     slots = (j % dilation * per_class + place // QUERY_COLS) * QUERY_COLS + place % QUERY_COLS
-    return table.reshape(-1), slots.astype(jnp.int32)
+    slots = slots[None, :] * rows + jnp.arange(rows, dtype=jnp.int32)[:, None]
+    return table.reshape(-1), slots.reshape(rows * cols, 1).astype(jnp.int32)
 
 
 def bias_tables(rel_bias, pattern, radius, dilation, rows):
@@ -416,73 +589,17 @@
     return bias.reshape(-1), step.astype(jnp.int32)
 
 
-def edge_spread(rows, cols):
-    spill = HALO - rows
-    span = cols + 2 * HALO
-    edge = spill * cols
-    side = -(-spill * HALO // 16) * 16
-    wide = edge + 2 * side
-    kept = side // spill
-    target = lax.broadcasted_iota(jnp.int32, (span * rows, 2 * wide), 0)
-    packed = lax.broadcasted_iota(jnp.int32, (span * rows, 2 * wide), 1)
-    at, extra = target // rows, target % rows
-    near, place = packed // wide, packed % wide
-    column, line = place // spill, place % spill
-    column = jnp.where(
-        place < edge,
-        column + HALO,
-        jnp.where(
-            place < edge + side,
-            column - cols + HALO - kept,
-            column - cols - kept + HALO + cols,
-        ),
-    )
-    hit = (at == column) & (extra == near * spill + line)
-    return hit.astype(jnp.bfloat16)
-
-
 def shards(
     query_map, key_map, value_map, window_mask, tile_radius, dilation_per_tile, rel_bias, out_weight
 ):
     rows, cols, features = query_map.shape
-    groups = features // GROUP_FEATURES
-    spill = HALO - rows
     dilation = dilation_per_tile[0, 0]
     table, slots = block_tables(dilation, rows, cols)
     bias, step = bias_tables(rel_bias, window_mask[0, 0], tile_radius[0, 0], dilation, rows)
-
-    pair = jnp.stack([key_map, value_map]).reshape(2, rows, cols, groups, GROUP_FEATURES)
-    kv = pair.transpose(3, 0, 2, 1, 4)
-    ends = jnp.stack([pair[:, :spill], pair[:, rows - spill :]])
-    edges = ends.transpose(4, 1, 0, 3, 2, 5).reshape(
-        groups, 2, 2, cols * spill, GROUP_FEATURES
-    )
-    query = query_map.transpose(1, 0, 2) * jnp.bfloat16(1.0 / math.sqrt(HEAD_DIM))
-    attended = fused_attention(
-        table, slots, bias, step, edge_spread(rows, cols), query, kv, edges
-    ).reshape(cols * rows, features)
-
-    count = lax.axis_size("head")
-    model = out_weight.shape[1]
-    if count != 2:
-        partials = jnp.dot(attended, out_weight, preferred_element_type=jnp.float32)
-        mixed = lax.psum_scatter(partials, "head", scatter_dimension=1, tiled=True)
-        mixed = mixed.astype(jnp.bfloat16).reshape(cols, rows, model // count)
-        return mixed.transpose(1, 0, 2)
-    me = lax.axis_index("head")
-    half = model // 2
-    theirs = lax.dynamic_slice_in_dim(out_weight, (1 - me) * half, half, 1)
-    mine = lax.dynamic_slice_in_dim(out_weight, me * half, half, 1)
-    mixed = []
-    parts = 2
-    tokens = rows * cols // parts
-    for part in range(parts):
-        block = attended[part * tokens : (part + 1) * tokens]
-        sent = jnp.dot(block, theirs, preferred_element_type=jnp.float32).astype(jnp.bfloat16)
-        got = lax.ppermute(sent, "head", [(0, 1), (1, 0)])
-        kept = jnp.dot(block, mine, preferred_element_type=jnp.float32)
-        mixed.append((kept + got.astype(jnp.float32)).astype(jnp.bfloat16))
-    return jnp.concatenate(mixed).reshape(cols, rows, half).transpose(1, 0, 2)
+    mixed = fused_layer(
+        table, bias, step, slots, query_map, key_map, value_map, out_weight
+    )
+    return mixed.reshape(rows, cols, out_weight.shape[1] // 2)
 
 
 def solution(mesh):

time: 168 us -> 122 us (0.73)
  the two profiles are of different devices: /device:TPU:1 before, /device:TPU:0 now
where the time goes in v2:
time: 122 us; the launch traced here: 121 us
  Pallas kernels  111 us (91%)
  local copies, waits for them, and re-layouts  5.63 us (5%)
  other arithmetic  3.2 us (3%)
  between operations  1.47 us (1%)
    pallas_call x1, Pallas kernels, fused_layer(): pl.pallas_call(functools.partial(fused_kernel, groups, rows, cols), in_sp...  111 us
    unnamed x2, local copies, waits for them, and re-layouts  2.86 us

profile of v2, /device:TPU:0, one launch (start us, length us, event | category | flops | bytes accessed | tf_op | source)
XLA Modules:
  0.0 121.3 jit_solution(15809833389134130857)
XLA Ops:
  1.4 0.1 multiply_add_fusion
  1.5 0.1 fusion.21
  1.7 0.1 fusion.12
  1.8 0.1 slice.7
  1.9 0.1 slice.6
  2.0 0.8 fusion.7.step_ref
  2.8 0.7 broadcast_compare_fusion
  3.5 0.1 fusion.18
  3.6 0.1 fusion.4
  3.7 0.1 add_clamp_fusion
  3.8 0.1 pad_add_fusion
  3.8 0.7 reshape.205.table_ref
  4.5 1.0 broadcast_select_fusion
  5.5 0.2 copy.12
  5.7 0.1 pad.9.clone
  5.8 0.8 reshape.206.bias_ref
  6.6 1.0 add.250.slot_ref
  7.6 111.0 %shard_map.82 = bf16[512,1536]{1,0:T(8,128)(2,1)} custom-call(s32[364]{0:T(512)} %reshape.205.table_ref, f32[5928]{0:T(1024)} %reshape.206.bias_ref, s32[16,128]{1,0:T(8,128)} %fusion.7.step_ref, s32[512,1]{1,0:T(8,128)} %add.250.slot_ref, bf16[16,32,1536]{2,1,0:T(8,128)(2,1)} %query_ref.1, bf16[16,32,1536]{2,1,0:T(8,128)(2,1)} %key_ref.1, ...), custom_call_target="tpu_custom_call" | custom-call | flops 14495514624 | bytes 6291456 | tf_op jit(solution)/shard_map/pallas_call | solution.py:487
  118.6 2.7 %copy.17 = bf16[16,32,1536]{2,1,0:T(8,128)(2,1)} copy(bf16[16,32,1536]{2,1,0:T(8,128)(2,1)} %bitcast.21) | data formatting | bytes 3145728
  (8 shorter events, 0.0 us)

commit v3 on v2

--- a/solution.py
+++ b/solution.py
@@ -41,7 +41,7 @@
 
 
 def fused_kernel(
-    groups, rows, cols, table_ref, bias_ref, step_ref, slot_ref, query_ref, key_ref, value_ref,
+    groups, rows, cols, dilation_ref, table_ref, bias_ref, query_ref, key_ref, value_ref,
     weight_hbm, out_ref, *scratch
 ):
     kv_refs, edge_refs = scratch[:groups], scratch[groups : 2 * groups]
@@ -252,8 +252,51 @@
         lax.broadcasted_iota(jnp.int32, (QUERY_COLS * rows, GROUP_FEATURES), 1) // HEAD_DIM
     )
 
+    def by_dilation(values):
+        chosen = values[DILATION_LIMIT]
+        for d in range(1, DILATION_LIMIT):
+            chosen = jnp.where(dilation_ref[0] == d, values[d], chosen)
+        return chosen
+
+    def window_step():
+        shape = (rows, 8 * rows)
+        spot = iota(shape, 1) % (4 * rows)
+        extra = spot - 3 * rows
+        offset = jnp.where(
+            spot < rows,
+            spot,
+            jnp.where(
+                spot < 2 * rows,
+                spot - 2 * rows,
+                jnp.where(
+                    spot < 3 * rows,
+                    spot - rows,
+                    jnp.where(extra < spill, extra - HALO, extra - spill + 2 * rows),
+                ),
+            ),
+        )
+        anchor = row * rows
+        real = (extra < 2 * spill) & (offset + anchor >= 0) & (offset + anchor < n_row * rows)
+        far = offset - iota(shape, 0)
+        lift = DILATION_LIMIT * 2 * HALO
+        steps = {}
+        for d in range(1, DILATION_LIMIT + 1):
+            hit = ((far + lift) % d == 0) & (jnp.abs(far) <= RADIUS_MAX * d)
+            steps[d] = jnp.where(hit, (far + lift) // d - lift // d + RADIUS_MAX, -1)
+        return jnp.where(real, by_dilation(steps), -1)
+
+    def column_slots(shape):
+        token = iota(shape, 0)
+        line, column = token // cols, token % cols
+        slots = {}
+        for d in range(1, DILATION_LIMIT + 1):
+            per_class = -(-(-(-cols // d)) // QUERY_COLS)
+            at = column // d
+            slots[d] = (column % d * per_class + at // QUERY_COLS) * QUERY_COLS + at % QUERY_COLS
+        return by_dilation(slots) * rows + line
+
     def build_bias(g):
-        step = step_ref[...]
+        step = window_step()
         masked = jnp.full(step.shape, MASKED, jnp.float32)
 
         def one(n, carry):
@@ -394,7 +437,7 @@
     wanted = jnp.where(second_half, spill, 0) + spot % spill
     spread_ref[...] = ((at == column) & (line == wanted)).astype(jnp.float32).astype(jnp.bfloat16)
     place_ref[...] = (
-        iota(place_ref.shape, 1) == jnp.broadcast_to(slot_ref[...], place_ref.shape)
+        iota(place_ref.shape, 1) == jnp.broadcast_to(column_slots((tokens, 1)), place_ref.shape)
     ).astype(jnp.float32).astype(jnp.bfloat16)
     for g in range(2, groups):
         turn(g)
@@ -417,7 +460,7 @@
 
         lax.fori_loop(0, model_tiles, one, 0)
 
-    pass_on, pass_last = min(2, groups - 1), min(4, groups - 1)
+    pass_on, pass_last = min(2, groups - 1), min(5, groups - 1)
     for g in range(groups):
         if g > 0:
             head_copy(g - 1).start()
@@ -443,21 +486,29 @@
     head_copy(groups - 1).start()
     swap_copy(SWAP_MATE).wait_recv()
     swap_copy(SWAP_LAST).wait_recv()
-    for g in range(groups):
+
+    def combine(before, done):
+        def one(n, carry):
+            lanes = pl.ds(pl.multiple_of(n * GROUP_FEATURES, GROUP_FEATURES), GROUP_FEATURES)
+            total = sum_ref[:, lanes]
+            for g in before:
+                weights = slice(g * GROUP_FEATURES, (g + 1) * GROUP_FEATURES)
+                total = total + jnp.dot(
+                    other_ref[g], theirs_ref[weights, lanes], preferred_element_type=jnp.float32
+                )
+            if done:
+                out_ref[:, lanes] = total.astype(jnp.bfloat16)
+            else:
+                sum_ref[:, lanes] = total
+            return carry
+
+        lax.fori_loop(0, model_tiles, one, 0)
+
+    for g in range(groups - 1):
         head_copy(g).wait_recv()
-
-    def last(n, carry):
-        lanes = pl.ds(pl.multiple_of(n * GROUP_FEATURES, GROUP_FEATURES), GROUP_FEATURES)
-        total = sum_ref[:, lanes]
-        for g in range(groups):
-            weights = slice(g * GROUP_FEATURES, (g + 1) * GROUP_FEATURES)
-            total = total + jnp.dot(
-                other_ref[g], theirs_ref[weights, lanes], preferred_element_type=jnp.float32
-            )
-        out_ref[:, lanes] = total.astype(jnp.bfloat16)
-        return carry
-
-    lax.fori_loop(0, model_tiles, last, 0)
+    combine(range(groups - 1), False)
+    head_copy(groups - 1).wait_recv()
+    combine([groups - 1], True)
     for g in range(groups):
         for which in range(COPIES):
             @pl.when(sends[which])
@@ -468,7 +519,7 @@
         swap_copy(which).wait_send()
 
 
-def fused_layer(table, bias, step, slots, query, key, value, weight):
+def fused_layer(dilation, table, bias, query, key, value, weight):
     rows, cols, features = query.shape
     groups = features // GROUP_FEATURES
     tokens = rows * cols
@@ -486,7 +537,7 @@
     half_type = jnp.bfloat16
     return pl.pallas_call(
         functools.partial(fused_kernel, groups, rows, cols),
-        in_specs=[smem, smem, vmem, vmem, vmem, vmem, vmem, hbm],
+        in_specs=[smem, smem, smem, vmem, vmem, vmem, hbm],
         out_specs=vmem,
         out_shape=jax.ShapeDtypeStruct((tokens, half), half_type),
         scratch_shapes=[
@@ -526,7 +577,7 @@
             bytes_accessed=query.size * 8,
             transcendentals=groups * blocks * stacked * keys,
         ),
-    )(table, bias, step, slots, query, key, value, weight)
+    )(dilation, table, bias, query, key, value, weight)
 
 
 def block_tables(dilation, rows, cols):
@@ -547,16 +598,10 @@
     key_cols = jnp.clip(key_cols + HALO, 0, span - 1)
     table = jnp.concatenate([query_cols, key_cols, kind], axis=1).astype(jnp.int32)
     table = jnp.pad(table, ((LEAD, TRAIL), (0, 0)))
-    j = jnp.arange(cols, dtype=jnp.int32)
-    place = j // dilation
-    slots = (j % dilation * per_class + place // QUERY_COLS) * QUERY_COLS + place % QUERY_COLS
-    slots = slots[None, :] * rows + jnp.arange(rows, dtype=jnp.int32)[:, None]
-    return table.reshape(-1), slots.reshape(rows * cols, 1).astype(jnp.int32)
-
-
-def bias_tables(rel_bias, pattern, radius, dilation, rows):
-    total_rows = rows * lax.axis_size("row")
-    anchor = lax.axis_index("row") * rows
+    return table.reshape(-1)
+
+
+def bias_tables(rel_bias, pattern, radius):
     steps = jnp.arange(WINDOW, dtype=jnp.int32) - RADIUS_MAX
     chosen = (pattern == 1) | ((steps[:, None] == 0) & (steps[None, :] == 0))
     chosen = chosen & (jnp.abs(steps)[:, None] <= radius) & (jnp.abs(steps)[None, :] <= radius)
@@ -565,28 +610,7 @@
     bias = jnp.pad(
         bias, ((0, 0), (0, 0), (before, TABLE_STEPS - WINDOW - before)), constant_values=MASKED
     )
-    spill = HALO - rows
-    i = lax.broadcasted_iota(jnp.int32, (rows, 8 * rows), 0)
-    spot = lax.broadcasted_iota(jnp.int32, (rows, 8 * rows), 1) % (4 * rows)
-    extra = spot - 3 * rows
-    offset = jnp.where(
-        spot < rows,
-        spot,
-        jnp.where(
-            spot < 2 * rows,
-            spot - 2 * rows,
-            jnp.where(
-                spot < 3 * rows,
-                spot - rows,
-                jnp.where(extra < spill, extra - HALO, extra - spill + 2 * rows),
-            ),
-        ),
-    )
-    real = (extra < 2 * spill) & (offset + anchor >= 0) & (offset + anchor < total_rows)
-    far = offset - i
-    hit = real & (far % dilation == 0) & (jnp.abs(far) <= RADIUS_MAX * dilation)
-    step = jnp.where(hit, far // dilation + RADIUS_MAX, -1)
-    return bias.reshape(-1), step.astype(jnp.int32)
+    return bias.reshape(-1)
 
 
 def shards(
@@ -594,10 +618,10 @@
 ):
     rows, cols, features = query_map.shape
     dilation = dilation_per_tile[0, 0]
-    table, slots = block_tables(dilation, rows, cols)
-    bias, step = bias_tables(rel_bias, window_mask[0, 0], tile_radius[0, 0], dilation, rows)
+    table = block_tables(dilation, rows, cols)
+    bias = bias_tables(rel_bias, window_mask[0, 0], tile_radius[0, 0])
     mixed = fused_layer(
-        table, bias, step, slots, query_map, key_map, value_map, out_weight
+        dilation.reshape(1), table, bias, query_map, key_map, value_map, out_weight
     )
     return mixed.reshape(rows, cols, out_weight.shape[1] // 2)
 

time: 122 us -> 109 us (0.89)
  Pallas kernels: 111 us -> 100 us
    pallas_call x1, Pallas kernels: 111 us -> 100 us  [fused_layer(): pl.pallas_call(functools.partial(fused_kernel, groups, rows, cols), in_sp...]
where the time goes in v3:
time: 109 us; the launch traced here: 108 us
  Pallas kernels  100 us (92%)
  local copies, waits for them, and re-layouts  4.67 us (4%)
  other arithmetic  2.23 us (2%)
  between operations  1.44 us (1%)
    pallas_call x1, Pallas kernels, fused_layer(): pl.pallas_call(functools.partial(fused_kernel, groups, rows, cols), in_sp...  100 us
    unnamed x2, local copies, waits for them, and re-layouts  2.86 us

profile of v3, /device:TPU:0, one launch (start us, length us, event | category | flops | bytes accessed | tf_op | source)
XLA Modules:
  0.0 108.4 jit_solution(11332755423229231626)
XLA Ops:
  1.4 0.1 multiply_add_fusion
  1.5 0.1 fusion.3
  1.6 0.1 slice.7
  1.7 0.1 slice.6
  1.8 0.7 broadcast_compare_fusion
  2.5 0.1 fusion.5
  2.6 0.1 fusion.2
  2.7 0.1 add_clamp_fusion
  2.8 0.1 pad_add_fusion
  2.9 0.7 reshape.129.table_ref
  3.5 1.0 broadcast_select_fusion
  4.5 0.2 copy.11
  4.7 0.1 pad.9.clone
  4.8 0.8 reshape.130.bias_ref
  5.6 100.1 %shard_map.82 = bf16[512,1536]{1,0:T(8,128)(2,1)} custom-call(s32[1]{0:T(128)} %bitcast.11.dilation_ref, s32[364]{0:T(512)} %reshape.129.table_ref, f32[5928]{0:T(1024)} %reshape.130.bias_ref, bf16[16,32,1536]{2,1,0:T(8,128)(2,1)} %query_ref.1, bf16[16,32,1536]{2,1,0:T(8,128)(2,1)} %key_ref.1, bf16[16,32,1536]{2,1,0:T(8,128)(2,1)} %value_ref.1, ...), custom_call_target="tpu_custom_call" | custom-call | flops 14495514624 | bytes 6291456 | tf_op jit(solution)/shard_map/pallas_call | solution.py:538
  105.7 2.7 %copy.16 = bf16[16,32,1536]{2,1,0:T(8,128)(2,1)} copy(bf16[16,32,1536]{2,1,0:T(8,128)(2,1)} %bitcast.18) | data formatting | bytes 3145728
  (5 shorter events, 0.0 us)
